TPU v7x, 8 devices: a whole 2x2x1 slice. The times are simulated.
8 devices in a mesh: inner: 4 (over z, y, x), data: 2 (over core).
Axes of the slice: x: 2, y: 2, z: 1, core: 2. Of those that a mesh axis runs over, the one named last changes fastest.
Arguments:
- x_t: bfloat16 [8, 576, 192], P(('inner', 'data'))
- labels_t: int32 [8], P(('inner', 'data'))
- x_next: bfloat16 [8, 576, 192], P(('inner', 'data'))
- w_in: float32 [8, 192, 768], replicated
- w_out: float32 [8, 768, 192], replicated
- w_head: float32 [192, 1000], replicated
- mom_in: float32 [8, 192, 768], replicated
- mom_out: float32 [8, 768, 192], replicated
- mom_head: float32 [192, 1000], replicated
- learn_rate: float32 [], replicated
- mom_coef: float32 [], replicated
Outputs:
- output 1: float32 [8, 1000], P(('inner', 'data'))
- output 2: float32 [8, 192, 768], replicated
- output 3: float32 [8, 768, 192], replicated
- output 4: float32 [192, 1000], replicated
- output 5: float32 [8, 192, 768], replicated
- output 6: float32 [8, 768, 192], replicated
- output 7: float32 [192, 1000], replicated
All inputs are finite; a program needn't handle non-finite values.
Results may differ from a plain program's by a relative error of at most 0.0121227.
Values are sent between devices in bfloat16 or wider.
A program may use at most 1 GiB of HBM per device.

v0:
```python
import jax
import jax.numpy as jnp
from jax import lax
from jax.sharding import PartitionSpec as P

LN_EPS = 1e-6
BATCH_AXES = ("inner", "data")


def layer_norm(stream):
    mean_val = jnp.mean(stream, axis=-1, keepdims=True)
    centered = stream - mean_val
    variance = jnp.mean(centered * centered, axis=-1, keepdims=True)
    return centered * lax.rsqrt(variance + LN_EPS)


def gelu_tanh(pre_act):
    return jax.nn.gelu(pre_act, approximate=True)


def forward_logits(tokens, in_bf, out_bf, head_bf):
    stream = tokens.astype(jnp.float32)
    for layer_idx in range(in_bf.shape[0]):
        act_in = layer_norm(stream).astype(jnp.bfloat16)
        pre_act = jnp.einsum("bsd,df->bsf", act_in, in_bf[layer_idx], preferred_element_type=jnp.float32)
        hidden = gelu_tanh(pre_act).astype(jnp.bfloat16)
        stream = stream + jnp.einsum("bsf,fd->bsd", hidden, out_bf[layer_idx], preferred_element_type=jnp.float32)
    pooled = jnp.mean(stream, axis=1).astype(jnp.bfloat16)
    return jnp.dot(pooled, head_bf, preferred_element_type=jnp.float32)


def local_backward(tokens, labels, in_bf, out_bf, head_bf, batch_total):
    stream = tokens.astype(jnp.float32)
    saved_acts = []
    for layer_idx in range(in_bf.shape[0]):
        act_in = layer_norm(stream).astype(jnp.bfloat16)
        pre_act = jnp.einsum("bsd,df->bsf", act_in, in_bf[layer_idx], preferred_element_type=jnp.float32)
        hidden = gelu_tanh(pre_act).astype(jnp.bfloat16)
        saved_acts.append((stream, act_in, pre_act, hidden))
        stream = stream + jnp.einsum("bsf,fd->bsd", hidden, out_bf[layer_idx], preferred_element_type=jnp.float32)
    pooled = jnp.mean(stream, axis=1).astype(jnp.bfloat16)
    logits = jnp.dot(pooled, head_bf, preferred_element_type=jnp.float32)
    targets = jax.nn.one_hot(labels, logits.shape[-1], dtype=jnp.float32)
    d_logits = ((jax.nn.softmax(logits, axis=-1) - targets) / batch_total).astype(jnp.bfloat16)
    grad_head = jnp.einsum("bd,bc->dc", pooled, d_logits, preferred_element_type=jnp.float32)
    d_pooled = jnp.einsum("bc,dc->bd", d_logits, head_bf, preferred_element_type=jnp.float32)
    d_pooled = d_pooled.astype(jnp.bfloat16).astype(jnp.float32) / stream.shape[1]
    d_stream = jnp.broadcast_to(d_pooled[:, None, :], stream.shape)
    grads_in = []
    grads_out = []
    for layer_idx in reversed(range(len(saved_acts))):
        stream_in, act_in, pre_act, hidden = saved_acts[layer_idx]
        d_branch = d_stream.astype(jnp.bfloat16)
        grads_out.insert(0, jnp.einsum("bsf,bsd->fd", hidden, d_branch, preferred_element_type=jnp.float32))
        d_hidden = jnp.einsum("bsd,fd->bsf", d_branch, out_bf[layer_idx], preferred_element_type=jnp.float32).astype(jnp.bfloat16)
        gelu_back = jax.vjp(gelu_tanh, pre_act)[1]
        d_pre = gelu_back(d_hidden.astype(jnp.float32))[0].astype(jnp.bfloat16)
        grads_in.insert(0, jnp.einsum("bsd,bsf->df", act_in, d_pre, preferred_element_type=jnp.float32))
        d_act = jnp.einsum("bsf,df->bsd", d_pre, in_bf[layer_idx], preferred_element_type=jnp.float32).astype(jnp.bfloat16)
        norm_back = jax.vjp(layer_norm, stream_in)[1]
        d_stream = d_stream + norm_back(d_act.astype(jnp.float32))[0]
    return grad_head, grads_in, grads_out


def reduce_grad(local_grad):
    wire_grad = local_grad.astype(jnp.bfloat16)
    grad_shard = lax.psum_scatter(wire_grad, "inner", scatter_dimension=0, tiled=True)
    grad_shard = lax.psum(grad_shard, "data")
    return lax.all_gather(grad_shard, "inner", axis=0, tiled=True).astype(jnp.float32)


def solution(mesh):
    batch_spec = P(BATCH_AXES)
    repl_spec = P()
    n_shards = mesh.shape["inner"] * mesh.shape["data"]

    def device_step(x_t, labels_t, x_next, w_in, w_out, w_head, mom_in, mom_out, mom_head, learn_rate, mom_coef):
        batch_total = x_t.shape[0] * n_shards
        grad_head, grads_in, grads_out = local_backward(x_t, labels_t, w_in.astype(jnp.bfloat16), w_out.astype(jnp.bfloat16), w_head.astype(jnp.bfloat16), batch_total)
        sum_head = reduce_grad(grad_head)
        in_sums = []
        out_sums = []
        for layer_idx in reversed(range(len(grads_in))):
            out_sums.insert(0, reduce_grad(grads_out[layer_idx]))
            in_sums.insert(0, reduce_grad(grads_in[layer_idx]))
        new_mom_in = mom_coef * mom_in + jnp.stack(in_sums)
        new_mom_out = mom_coef * mom_out + jnp.stack(out_sums)
        new_mom_head = mom_coef * mom_head + sum_head
        new_w_in = w_in - learn_rate * new_mom_in
        new_w_out = w_out - learn_rate * new_mom_out
        new_w_head = w_head - learn_rate * new_mom_head
        logits_next = forward_logits(x_next, new_w_in.astype(jnp.bfloat16), new_w_out.astype(jnp.bfloat16), new_w_head.astype(jnp.bfloat16))
        return logits_next, new_w_in, new_w_out, new_w_head, new_mom_in, new_mom_out, new_mom_head

    return jax.shard_map(device_step, mesh=mesh, in_specs=(batch_spec, batch_spec, batch_spec) + (repl_spec,) * 8, out_specs=(batch_spec,) + (repl_spec,) * 6, check_vma=False)
```

profile of v0, /device:TPU:0, one launch (start us, length us, event | category | flops | bytes accessed | tf_op | source)
XLA Modules:
  0.0 661.3 jit_solution(12181885564420994721)
XLA Ops:
  9.9 2.7 convert_element_type.440
  45.8 3.0 convolution_convert_fusion.8
  49.4 3.0 fusion.2
  59.3 3.2 fusion.7
  69.9 3.1 fusion.12
  80.4 3.1 fusion.17
  90.8 3.1 fusion.22
  101.1 2.9 fusion.27
  114.0 3.1 convolution_convert_fusion.14
  122.3 3.3 fusion.169
  126.6 9.0 %reduce-scatter.30.cloned.1.call-done = bf16[48,768]{1,0:T(8,128)(2,1)} async-done(((bf16[192,768]{1,0:T(8,128)(2,1)}), bf16[48,768]{1,0:T(8,128)(2,1)}) %reduce-scatter.30.cloned.1.call-update) | async-done | bytes 73744 | tf_op jit(solution)/shard_map/reduce_scatter | solution.py:67
  135.7 21.6 %reduce-scatter.44.cloned.1.call-done = bf16[192,192]{1,0:T(8,128)(2,1)} async-done(((bf16[768,192]{1,0:T(8,128)(2,1)}), bf16[192,192]{1,0:T(8,128)(2,1)}) %reduce-scatter.44.cloned.1.call-update) | async-done | bytes 73744 | tf_op jit(solution)/shard_map/reduce_scatter | solution.py:67
  157.3 21.4 %reduce-scatter.28.cloned.1.call-done = bf16[48,768]{1,0:T(8,128)(2,1)} async-done(((bf16[192,768]{1,0:T(8,128)(2,1)}), bf16[48,768]{1,0:T(8,128)(2,1)}) %reduce-scatter.28.cloned.1.call-update) | async-done | bytes 73744 | tf_op jit(solution)/shard_map/reduce_scatter | solution.py:67
  178.7 21.7 %reduce-scatter.42.cloned.1.call-done = bf16[192,192]{1,0:T(8,128)(2,1)} async-done(((bf16[768,192]{1,0:T(8,128)(2,1)}), bf16[192,192]{1,0:T(8,128)(2,1)}) %reduce-scatter.42.cloned.1.call-update) | async-done | bytes 73744 | tf_op jit(solution)/shard_map/reduce_scatter | solution.py:67
  200.4 21.6 %reduce-scatter.26.cloned.1.call-done = bf16[48,768]{1,0:T(8,128)(2,1)} async-done(((bf16[192,768]{1,0:T(8,128)(2,1)}), bf16[48,768]{1,0:T(8,128)(2,1)}) %reduce-scatter.26.cloned.1.call-update) | async-done | bytes 73744 | tf_op jit(solution)/shard_map/reduce_scatter | solution.py:67
  222.0 21.7 %reduce-scatter.40.cloned.1.call-done = bf16[192,192]{1,0:T(8,128)(2,1)} async-done(((bf16[768,192]{1,0:T(8,128)(2,1)}), bf16[192,192]{1,0:T(8,128)(2,1)}) %reduce-scatter.40.cloned.1.call-update) | async-done | bytes 73744 | tf_op jit(solution)/shard_map/reduce_scatter | solution.py:67
  243.7 21.4 %reduce-scatter.24.cloned.1.call-done = bf16[48,768]{1,0:T(8,128)(2,1)} async-done(((bf16[192,768]{1,0:T(8,128)(2,1)}), bf16[48,768]{1,0:T(8,128)(2,1)}) %reduce-scatter.24.cloned.1.call-update) | async-done | bytes 73744 | tf_op jit(solution)/shard_map/reduce_scatter | solution.py:67
  265.1 22.3 %reduce-scatter.38.cloned.1.call-done = bf16[192,192]{1,0:T(8,128)(2,1)} async-done(((bf16[768,192]{1,0:T(8,128)(2,1)}), bf16[192,192]{1,0:T(8,128)(2,1)}) %reduce-scatter.38.cloned.1.call-update) | async-done | bytes 73744 | tf_op jit(solution)/shard_map/reduce_scatter | solution.py:67
  287.5 21.4 %reduce-scatter.22.cloned.1.call-done = bf16[48,768]{1,0:T(8,128)(2,1)} async-done(((bf16[192,768]{1,0:T(8,128)(2,1)}), bf16[48,768]{1,0:T(8,128)(2,1)}) %reduce-scatter.22.cloned.1.call-update) | async-done | bytes 73744 | tf_op jit(solution)/shard_map/reduce_scatter | solution.py:67
  308.9 22.1 %reduce-scatter.20.cloned.1.call-done = bf16[48,768]{1,0:T(8,128)(2,1)} async-done(((bf16[192,768]{1,0:T(8,128)(2,1)}), bf16[48,768]{1,0:T(8,128)(2,1)}) %reduce-scatter.20.cloned.1.call-update) | async-done | bytes 73744 | tf_op jit(solution)/shard_map/reduce_scatter | solution.py:67
  331.0 22.2 %reduce-scatter.36.cloned.1.call-done = bf16[192,192]{1,0:T(8,128)(2,1)} async-done(((bf16[768,192]{1,0:T(8,128)(2,1)}), bf16[192,192]{1,0:T(8,128)(2,1)}) %reduce-scatter.36.cloned.1.call-update) | async-done | bytes 73744 | tf_op jit(solution)/shard_map/reduce_scatter | solution.py:67
  353.2 22.2 %reduce-scatter.34.cloned.1.call-done = bf16[192,192]{1,0:T(8,128)(2,1)} async-done(((bf16[768,192]{1,0:T(8,128)(2,1)}), bf16[192,192]{1,0:T(8,128)(2,1)}) %reduce-scatter.34.cloned.1.call-update) | async-done | bytes 73744 | tf_op jit(solution)/shard_map/reduce_scatter | solution.py:67
  375.3 22.0 %reduce-scatter.18.cloned.1.call-done = bf16[48,768]{1,0:T(8,128)(2,1)} async-done(((bf16[192,768]{1,0:T(8,128)(2,1)}), bf16[48,768]{1,0:T(8,128)(2,1)}) %reduce-scatter.18.cloned.1.call-update) | async-done | bytes 73744 | tf_op jit(solution)/shard_map/reduce_scatter | solution.py:67
  397.3 22.2 %reduce-scatter.50.cloned.1.call-done = bf16[48,1000]{1,0:T(8,128)(2,1)} async-done(((bf16[192,1000]{1,0:T(8,128)(2,1)}), bf16[48,1000]{1,0:T(8,128)(2,1)}) %reduce-scatter.50.cloned.1.call-update) | async-done | bytes 96016 | tf_op jit(solution)/shard_map/reduce_scatter | solution.py:67
  419.5 6.2 copy.19
  427.0 6.3 copy.18
  433.5 6.1 all-reduce.3.cloned.1.call-done
  439.5 10.2 %all_gather.59 = bf16[768,192]{1,0:T(8,128)(2,1)S(1)} all-gather(bf16[192,192]{1,0:T(8,128)(2,1)} %get-tuple-element.14), channel_id=1, replica_groups=mesh['inner'=4,'data'=2] {'inner'}, dimensions={0}, use_global_device_ids=true | all-gather | bytes 368640 | tf_op jit(solution)/shard_map/all_gather | solution.py:69
  449.8 9.0 %all_gather.51 = bf16[192,768]{1,0:T(8,128)(2,1)S(1)} all-gather(bf16[48,768]{1,0:T(8,128)(2,1)} %get-tuple-element.22), channel_id=1, replica_groups=mesh['inner'=4,'data'=2] {'inner'}, dimensions={0}, use_global_device_ids=true | all-gather | bytes 368640 | tf_op jit(solution)/shard_map/all_gather | solution.py:69
  458.8 9.2 %all_gather.52 = bf16[192,768]{1,0:T(8,128)(2,1)} all-gather(bf16[48,768]{1,0:T(8,128)(2,1)} %get-tuple-element.23), channel_id=1, replica_groups=mesh['inner'=4,'data'=2] {'inner'}, dimensions={0}, use_global_device_ids=true | all-gather | bytes 368640 | tf_op jit(solution)/shard_map/all_gather | solution.py:69
  468.0 9.2 %all_gather.53 = bf16[192,768]{1,0:T(8,128)(2,1)} all-gather(bf16[48,768]{1,0:T(8,128)(2,1)} %get-tuple-element.24), channel_id=1, replica_groups=mesh['inner'=4,'data'=2] {'inner'}, dimensions={0}, use_global_device_ids=true | all-gather | bytes 368640 | tf_op jit(solution)/shard_map/all_gather | solution.py:69
  477.3 9.1 %all_gather.54 = bf16[192,768]{1,0:T(8,128)(2,1)} all-gather(bf16[48,768]{1,0:T(8,128)(2,1)} %get-tuple-element.25), channel_id=1, replica_groups=mesh['inner'=4,'data'=2] {'inner'}, dimensions={0}, use_global_device_ids=true | all-gather | bytes 368640 | tf_op jit(solution)/shard_map/all_gather | solution.py:69
  486.4 8.8 %all_gather.55 = bf16[192,768]{1,0:T(8,128)(2,1)} all-gather(bf16[48,768]{1,0:T(8,128)(2,1)S(1)} %copy-done.78), channel_id=1, replica_groups=mesh['inner'=4,'data'=2] {'inner'}, dimensions={0}, use_global_device_ids=true | all-gather | bytes 368640 | tf_op jit(solution)/shard_map/all_gather | solution.py:69
  495.2 9.1 %all_gather.56 = bf16[192,768]{1,0:T(8,128)(2,1)} all-gather(bf16[48,768]{1,0:T(8,128)(2,1)S(1)} %copy-done.77), channel_id=1, replica_groups=mesh['inner'=4,'data'=2] {'inner'}, dimensions={0}, use_global_device_ids=true | all-gather | bytes 368640 | tf_op jit(solution)/shard_map/all_gather | solution.py:69
  504.3 9.0 %all_gather.57 = bf16[192,768]{1,0:T(8,128)(2,1)} all-gather(bf16[48,768]{1,0:T(8,128)(2,1)S(1)} %copy-done.76), channel_id=1, replica_groups=mesh['inner'=4,'data'=2] {'inner'}, dimensions={0}, use_global_device_ids=true | all-gather | bytes 368640 | tf_op jit(solution)/shard_map/all_gather | solution.py:69
  513.3 9.4 %all_gather.58 = bf16[192,768]{1,0:T(8,128)(2,1)} all-gather(bf16[48,768]{1,0:T(8,128)(2,1)S(1)} %copy-done.75), channel_id=1, replica_groups=mesh['inner'=4,'data'=2] {'inner'}, dimensions={0}, use_global_device_ids=true | all-gather | bytes 368640 | tf_op jit(solution)/shard_map/all_gather | solution.py:69
  522.7 9.1 %all_gather.60 = bf16[768,192]{1,0:T(8,128)(2,1)S(1)} all-gather(bf16[192,192]{1,0:T(8,128)(2,1)S(1)} %copy-done.74), channel_id=1, replica_groups=mesh['inner'=4,'data'=2] {'inner'}, dimensions={0}, use_global_device_ids=true | all-gather | bytes 368640 | tf_op jit(solution)/shard_map/all_gather | solution.py:69
  531.8 9.1 %all_gather.61 = bf16[768,192]{1,0:T(8,128)(2,1)S(1)} all-gather(bf16[192,192]{1,0:T(8,128)(2,1)S(1)} %copy-done.73), channel_id=1, replica_groups=mesh['inner'=4,'data'=2] {'inner'}, dimensions={0}, use_global_device_ids=true | all-gather | bytes 368640 | tf_op jit(solution)/shard_map/all_gather | solution.py:69
  540.9 9.3 %all_gather.62 = bf16[768,192]{1,0:T(8,128)(2,1)S(1)} all-gather(bf16[192,192]{1,0:T(8,128)(2,1)S(1)} %copy-done.72), channel_id=1, replica_groups=mesh['inner'=4,'data'=2] {'inner'}, dimensions={0}, use_global_device_ids=true | all-gather | bytes 368640 | tf_op jit(solution)/shard_map/all_gather | solution.py:69
  550.2 9.5 %all_gather.63 = bf16[768,192]{1,0:T(8,128)(2,1)S(1)} all-gather(bf16[192,192]{1,0:T(8,128)(2,1)S(1)} %copy-done.71), channel_id=1, replica_groups=mesh['inner'=4,'data'=2] {'inner'}, dimensions={0}, use_global_device_ids=true | all-gather | bytes 368640 | tf_op jit(solution)/shard_map/all_gather | solution.py:69
  559.8 9.6 %all_gather.64 = bf16[768,192]{1,0:T(8,128)(2,1)S(1)} all-gather(bf16[192,192]{1,0:T(8,128)(2,1)S(1)} %copy-done.70), channel_id=1, replica_groups=mesh['inner'=4,'data'=2] {'inner'}, dimensions={0}, use_global_device_ids=true | all-gather | bytes 368640 | tf_op jit(solution)/shard_map/all_gather | solution.py:69
  569.4 8.4 %all_gather.65 = bf16[768,192]{1,0:T(8,128)(2,1)S(1)} all-gather(bf16[192,192]{1,0:T(8,128)(2,1)S(1)} %copy-done.69), channel_id=1, replica_groups=mesh['inner'=4,'data'=2] {'inner'}, dimensions={0}, use_global_device_ids=true | all-gather | bytes 368640 | tf_op jit(solution)/shard_map/all_gather | solution.py:69
  577.8 9.6 %all_gather.66 = bf16[768,192]{1,0:T(8,128)(2,1)S(1)} all-gather(bf16[192,192]{1,0:T(8,128)(2,1)S(1)} %copy-done.68), channel_id=1, replica_groups=mesh['inner'=4,'data'=2] {'inner'}, dimensions={0}, use_global_device_ids=true | all-gather | bytes 368640 | tf_op jit(solution)/shard_map/all_gather | solution.py:69
  587.4 8.4 %all_gather.67 = bf16[192,1000]{1,0:T(8,128)(2,1)S(1)} all-gather(bf16[48,1000]{1,0:T(8,128)(2,1)S(1)} %copy-done.67), channel_id=1, replica_groups=mesh['inner'=4,'data'=2] {'inner'}, dimensions={0}, use_global_device_ids=true | all-gather | bytes 480000 | tf_op jit(solution)/shard_map/all_gather | solution.py:69
  596.9 11.8 %fusion.412 = (bf16[8,768,192]{2,1,0:T(8,128)(2,1)}, f32[8,768,192]{2,1,0:T(8,128)}, f32[8,768,192]{2,1,0:T(8,128)}) fusion(f32[8,768,192]{2,1,0:T(8,128)} %copy.19, f32[]{:T(128)S(6)} %copy.54, bf16[8,768,192]{2,1,0:T(8,128)(2,1)S(1)} %bitcast_dynamic-update-slice_fusion, f32[8,768,192]{2,1,0:T(8,128)} %copy.18, f32[]{:T(128)S(6)} %copy.55), kind=kLoop, calls=%fused_computation.607 | loop fusion | flops 7077888 | bytes 23592968 | tf_op jit(solution)/shard_map/convert_element_type | solution.py:92
  608.6 6.3 copy.20
  615.0 6.3 copy.21
  624.5 9.5 %fusion.411 = (bf16[8,192,768]{2,1,0:T(8,128)(2,1)}, f32[8,192,768]{2,1,0:T(8,128)}, f32[8,192,768]{2,1,0:T(8,128)}) fusion(f32[8,192,768]{2,1,0:T(8,128)} %param.14, f32[]{:T(128)S(6)} %copy.54, bf16[8,192,768]{2,1,0:T(8,128)(2,1)S(1)} %bitcast_dynamic-update-slice_fusion.8, f32[8,192,768]{2,1,0:T(8,128)} %param.17, f32[]{:T(128)S(6)} %copy.55), kind=kLoop, calls=%fused_computation.606 | loop fusion | flops 7077888 | bytes 23592968 | tf_op jit(solution)/shard_map/convert_element_type | solution.py:92
  (350 shorter events, 111.0 us)
Async XLA Ops:
  7.2 119.4 %reduce-scatter.48.cloned.1.call-start = ((), (), s32[]{:S(2)}) async-start(), calls=%async_computation.32 | async-start | bytes 491520 | tf_op jit(solution)/shard_map/reduce_scatter | solution.py:67
  9.9 3.8 copy-start.2
  16.9 3.6 copy-start.6
  24.0 3.6 copy-start.8
  31.1 3.6 copy-start.10
  34.7 3.6 copy-start.3
  38.3 3.8 copy-start.13
  48.9 77.7 %reduce-scatter.32.cloned.1.call-start = ((), (), s32[]{:S(2)}) async-start(), calls=%async_computation.24 | async-start | bytes 368640 | tf_op jit(solution)/shard_map/reduce_scatter | solution.py:67
  49.4 4.1 copy-start.14
  49.4 5.2 copy-start.1
  54.6 72.0 %reduce-scatter.46.cloned.1.call-start = ((), (), s32[]{:S(2)}) async-start(), calls=%async_computation.31 | async-start | bytes 491520 | tf_op jit(solution)/shard_map/reduce_scatter | solution.py:67
  59.3 76.4 %reduce-scatter.30.cloned.1.call-start = ((), (), s32[]{:S(2)}) async-start(), calls=%async_computation.23 | async-start | bytes 368640 | tf_op jit(solution)/shard_map/reduce_scatter | solution.py:67
  59.3 4.1 copy-start.4
  64.6 92.7 %reduce-scatter.44.cloned.1.call-start = ((), (), s32[]{:S(2)}) async-start(), calls=%async_computation.30 | async-start | bytes 491520 | tf_op jit(solution)/shard_map/reduce_scatter | solution.py:67
  69.8 108.8 %reduce-scatter.28.cloned.1.call-start = ((), (), s32[]{:S(2)}) async-start(), calls=%async_computation.22 | async-start | bytes 368640 | tf_op jit(solution)/shard_map/reduce_scatter | solution.py:67
  69.9 4.1 copy-start.11
  75.1 125.3 %reduce-scatter.42.cloned.1.call-start = ((), (), s32[]{:S(2)}) async-start(), calls=%async_computation.29 | async-start | bytes 491520 | tf_op jit(solution)/shard_map/reduce_scatter | solution.py:67
  80.3 141.6 %reduce-scatter.26.cloned.1.call-start = ((), (), s32[]{:S(2)}) async-start(), calls=%async_computation.21 | async-start | bytes 368640 | tf_op jit(solution)/shard_map/reduce_scatter | solution.py:67
  85.5 158.2 %reduce-scatter.40.cloned.1.call-start = ((), (), s32[]{:S(2)}) async-start(), calls=%async_computation.28 | async-start | bytes 491520 | tf_op jit(solution)/shard_map/reduce_scatter | solution.py:67
  90.8 4.1 copy-start.9
  90.8 174.4 %reduce-scatter.24.cloned.1.call-start = ((), (), s32[]{:S(2)}) async-start(), calls=%async_computation.20 | async-start | bytes 368640 | tf_op jit(solution)/shard_map/reduce_scatter | solution.py:67
  96.0 191.4 %reduce-scatter.38.cloned.1.call-start = ((), (), s32[]{:S(2)}) async-start(), calls=%async_computation.27 | async-start | bytes 491520 | tf_op jit(solution)/shard_map/reduce_scatter | solution.py:67
  101.0 207.8 %reduce-scatter.22.cloned.1.call-start = ((), (), s32[]{:S(2)}) async-start(), calls=%async_computation.19 | async-start | bytes 368640 | tf_op jit(solution)/shard_map/reduce_scatter | solution.py:67
  106.1 224.9 %reduce-scatter.20.cloned.1.call-start = ((), (), s32[]{:S(2)}) async-start(), calls=%async_computation.18 | async-start | bytes 368640 | tf_op jit(solution)/shard_map/reduce_scatter | solution.py:67
  109.3 3.5 copy-start.7
  113.9 239.2 %reduce-scatter.36.cloned.1.call-start = ((), (), s32[]{:S(2)}) async-start(), calls=%async_computation.26 | async-start | bytes 491520 | tf_op jit(solution)/shard_map/reduce_scatter | solution.py:67
  117.2 258.2 %reduce-scatter.34.cloned.1.call-start = ((), (), s32[]{:S(2)}) async-start(), calls=%async_computation.25 | async-start | bytes 491520 | tf_op jit(solution)/shard_map/reduce_scatter | solution.py:67
  122.0 275.3 %reduce-scatter.18.cloned.1.call-start = ((), (), s32[]{:S(2)}) async-start(), calls=%async_computation.17 | async-start | bytes 368640 | tf_op jit(solution)/shard_map/reduce_scatter | solution.py:67
  125.6 293.9 %reduce-scatter.50.cloned.1.call-start = ((), (), s32[]{:S(2)}) async-start(), calls=%async_computation.33 | async-start | bytes 491520 | tf_op jit(solution)/shard_map/reduce_scatter | solution.py:67
  126.5 313.0 %all-reduce.3.cloned.1.call-start = ((), (), s32[]{:S(2)}) async-start(), calls=%async_computation.34 | async-start | bytes 2949120 | tf_op jit(solution)/shard_map/psum | solution.py:68
  427.0 6.3 copy-start.63
  439.5 46.8 %copy-start.78 = (bf16[48,768]{1,0:T(8,128)(2,1)S(1)}, bf16[48,768]{1,0:T(8,128)(2,1)}, u32[]{:S(2)}) copy-start(bf16[48,768]{1,0:T(8,128)(2,1)} %get-tuple-element.26) | copy-start | bytes 221188
  439.5 55.7 %copy-start.77 = (bf16[48,768]{1,0:T(8,128)(2,1)S(1)}, bf16[48,768]{1,0:T(8,128)(2,1)}, u32[]{:S(2)}) copy-start(bf16[48,768]{1,0:T(8,128)(2,1)} %get-tuple-element.27) | copy-start | bytes 221188
  439.5 64.8 %copy-start.76 = (bf16[48,768]{1,0:T(8,128)(2,1)S(1)}, bf16[48,768]{1,0:T(8,128)(2,1)}, u32[]{:S(2)}) copy-start(bf16[48,768]{1,0:T(8,128)(2,1)} %get-tuple-element.28) | copy-start | bytes 221188
  439.5 73.7 %copy-start.75 = (bf16[48,768]{1,0:T(8,128)(2,1)S(1)}, bf16[48,768]{1,0:T(8,128)(2,1)}, u32[]{:S(2)}) copy-start(bf16[48,768]{1,0:T(8,128)(2,1)} %get-tuple-element.29) | copy-start | bytes 221188
  439.5 83.1 %copy-start.74 = (bf16[192,192]{1,0:T(8,128)(2,1)S(1)}, bf16[192,192]{1,0:T(8,128)(2,1)}, u32[]{:S(2)}) copy-start(bf16[192,192]{1,0:T(8,128)(2,1)} %get-tuple-element.15) | copy-start | bytes 221188
  449.8 82.0 %copy-start.73 = (bf16[192,192]{1,0:T(8,128)(2,1)S(1)}, bf16[192,192]{1,0:T(8,128)(2,1)}, u32[]{:S(2)}) copy-start(bf16[192,192]{1,0:T(8,128)(2,1)} %get-tuple-element.16) | copy-start | bytes 221188
  458.8 82.1 %copy-start.72 = (bf16[192,192]{1,0:T(8,128)(2,1)S(1)}, bf16[192,192]{1,0:T(8,128)(2,1)}, u32[]{:S(2)}) copy-start(bf16[192,192]{1,0:T(8,128)(2,1)} %get-tuple-element.17) | copy-start | bytes 221188
  468.0 82.2 %copy-start.71 = (bf16[192,192]{1,0:T(8,128)(2,1)S(1)}, bf16[192,192]{1,0:T(8,128)(2,1)}, u32[]{:S(2)}) copy-start(bf16[192,192]{1,0:T(8,128)(2,1)} %get-tuple-element.18) | copy-start | bytes 221188
  486.4 73.4 %copy-start.70 = (bf16[192,192]{1,0:T(8,128)(2,1)S(1)}, bf16[192,192]{1,0:T(8,128)(2,1)}, u32[]{:S(2)}) copy-start(bf16[192,192]{1,0:T(8,128)(2,1)} %get-tuple-element.19) | copy-start | bytes 221188
  495.2 74.2 %copy-start.69 = (bf16[192,192]{1,0:T(8,128)(2,1)S(1)}, bf16[192,192]{1,0:T(8,128)(2,1)}, u32[]{:S(2)}) copy-start(bf16[192,192]{1,0:T(8,128)(2,1)} %get-tuple-element.20) | copy-start | bytes 221188
  504.3 73.5 %copy-start.68 = (bf16[192,192]{1,0:T(8,128)(2,1)S(1)}, bf16[192,192]{1,0:T(8,128)(2,1)}, u32[]{:S(2)}) copy-start(bf16[192,192]{1,0:T(8,128)(2,1)} %get-tuple-element.21) | copy-start | bytes 221188
  522.7 64.7 %copy-start.67 = (bf16[48,1000]{1,0:T(8,128)(2,1)S(1)}, bf16[48,1000]{1,0:T(8,128)(2,1)}, u32[]{:S(2)}) copy-start(bf16[48,1000]{1,0:T(8,128)(2,1)} %get-tuple-element.30) | copy-start | bytes 288004
  615.0 6.3 copy-start.36
  621.2 3.1 copy-start.61
  621.2 3.1 copy-start.60
  621.2 3.2 copy-start.59
  624.5 9.5 %copy-start.64 = (bf16[1,576,192]{1,2,0:T(8,128)(2,1)S(1)}, bf16[1,576,192]{1,2,0:T(8,128)(2,1)}, u32[]{:S(2)}) copy-start(bf16[1,576,192]{1,2,0:T(8,128)(2,1)} %param.13) | copy-start | bytes 663556
  (49 other events, 81.9 us)
Sparse Core Ops, SparseCore 0:
  49.0 21.8 reduce-scatter.47
  73.6 18.8 reduce-scatter.31
  95.2 18.9 reduce-scatter.45
  116.8 18.8 reduce-scatter.29
  138.2 18.9 reduce-scatter.43
  159.8 18.8 reduce-scatter.27
  181.4 18.9 reduce-scatter.41
  203.1 18.8 reduce-scatter.25
  224.7 18.9 reduce-scatter.39
  246.3 18.8 reduce-scatter.23
  268.4 18.9 reduce-scatter.37
  290.0 18.8 reduce-scatter.21
  312.2 18.8 reduce-scatter.19
  334.2 18.9 reduce-scatter.35
  356.3 18.9 reduce-scatter.33
  378.5 18.8 reduce-scatter.17
  400.5 18.9 reduce-scatter.49
  422.9 16.5 all-reduce.2
where the time goes:
time: 672 us; the launch traced here: 661 us
  waiting for transfers between devices  299 us (44%)
  blocking collectives  156 us (23%)
  matrix products  104 us (15%)
  local copies, waits for them, and re-layouts  47.1 us (7%)
  other arithmetic  34.5 us (5%)
  between operations  18.2 us (3%)
    reduce_scatter x17, waiting for transfers between devices, reduce_grad(): lax.psum_scatter(wire_grad, 'inner', scatter_dimension=0, tiled=True)  293 us
    all_gather x17, blocking collectives, reduce_grad(): lax.all_gather(grad_shard, 'inner', axis=0, tiled=True).astype(jnp.float32)  156 us
    unnamed x176, local copies, waits for them, and re-layouts  47.1 us
    dot_general x7, matrix products, local_backward(): jnp.einsum('bsd,fd->bsf', d_branch, out_bf[layer_idx], preferred_element_...  21 us
    dot_general x8, matrix products, forward_logits(): jnp.einsum('bsf,fd->bsd', hidden, out_bf[layer_idx], preferred_element_ty...  17.4 us
    dot_general x8, matrix products, local_backward(): jnp.einsum('bsf,bsd->fd', hidden, d_branch, preferred_element_type=jnp.fl...  15.8 us
    dot_general x8, matrix products, local_backward(): jnp.einsum('bsf,fd->bsd', hidden, out_bf[layer_idx], preferred_element_ty...  14.8 us
  transfers between devices with their start and end apart: 18, of which 15 were waited for; matrix products, arithmetic and copies ran while one was open for 11% of the time, Pallas kernels for 0%

commit v1 on v0

v1 whole, which is shorter than its diff:
```python
import functools

import jax
import jax.numpy as jnp
from jax import lax
from jax.experimental import pallas as pl
from jax.experimental.pallas import tpu as pltpu
from jax.sharding import PartitionSpec as P

LN_EPS = 1e-6
BATCH_AXES = ("inner", "data")
MESH = pl.DeviceIdType.MESH
LANES = 128
GELU_SCALE = 0.7978845608028654
GELU_CUBIC = 0.044715
F32 = jnp.float32
BF16 = jnp.bfloat16
NT = (((1,), (1,)), ((), ()))
NN = (((1,), (0,)), ((), ()))
TN = (((0,), (0,)), ((), ()))
VMEM_BYTES = 66 * 1000 * 1000


def dot(a, b, dims):
    return lax.dot_general(a, b, dims, preferred_element_type=F32)


def normalize(stream):
    mean_val = jnp.mean(stream, axis=-1, keepdims=True)
    centered = stream - mean_val
    variance = jnp.mean(centered * centered, axis=-1, keepdims=True)
    rstd = lax.rsqrt(variance + LN_EPS)
    return centered * rstd, rstd


def step_kernel(n_shards, rows,
                x_ref, label_ref, w_in_hbm, w_out_hbm, w_head_ref,
                sums_hbm, head_sum_ref,
                stream, d_stream, x_hat, rstds, acts, hidden, d_gelu, d_branch, d_pre,
                w_in_f32, w_out_f32, w_in, w_out,
                grads, recv0, recv1, recv2, sums, head_send, head_recv,
                load_sem, store_sem, send_sem, recv_sem, head_send_sem, head_recv_sem):
    layers, tokens, mlp_dim = hidden.shape
    dim = stream.shape[1]
    classes = w_head_ref.shape[1]
    chunks = mlp_dim // LANES
    weight_rows = chunks * dim
    half = weight_rows
    quarter, eighth = half // 4, half // 8
    inner, core = lax.axis_index("inner"), lax.axis_index("data")
    y, x = inner // 2, inner % 2
    peer_core = (inner, 1 - core)
    peer_x = (inner + 1 - 2 * x, core)
    peer_y = (inner + 2 - 4 * y, core)
    barrier = pltpu.get_barrier_semaphore()
    me = inner * 2 + core
    for step in range(1, n_shards):
        other = (me + step) % n_shards
        pl.semaphore_signal(barrier, inc=1, device_id=(other // 2, other % 2), device_id_type=MESH)

    def load(layer, slot):
        return (pltpu.make_async_copy(w_in_hbm.at[layer], w_in_f32.at[slot], load_sem.at[slot, 0]),
                pltpu.make_async_copy(w_out_hbm.at[layer], w_out_f32.at[slot], load_sem.at[slot, 1]))

    for copy in load(0, 0):
        copy.start()
    stream[...] = x_ref[0].astype(F32).T

    def forward(layer, carry):
        slot = layer % 2

        @pl.when(layer + 1 < layers)
        def _():
            for copy in load(layer + 1, 1 - slot):
                copy.start()

        for copy in load(layer, slot):
            copy.wait()
        w_in[layer] = w_in_f32[slot].astype(BF16)
        w_out[layer] = w_out_f32[slot].astype(BF16)
        for start in range(0, tokens, rows):
            part = slice(start, start + rows)
            stream_in = stream[part]
            normed, rstd = normalize(stream_in)
            act = normed.astype(BF16)
            x_hat[layer, part] = normed
            rstds[layer, part] = rstd
            acts[layer, part] = act
            pre = dot(act, w_in[layer], NN)
            square = pre * pre
            tanh_val = jnp.tanh(pre * (GELU_SCALE + (GELU_SCALE * GELU_CUBIC) * square))
            cdf = 0.5 + 0.5 * tanh_val
            out = (pre * cdf).astype(BF16)
            slope = (0.5 * GELU_SCALE) + (1.5 * GELU_SCALE * GELU_CUBIC) * square
            d_gelu[layer, part] = cdf + (pre * slope) * (1.0 - tanh_val * tanh_val)
            hidden[layer, part] = out
            stream[part] = stream_in + dot(out, w_out[layer], NT)
        return carry

    lax.fori_loop(0, layers, forward, 0)

    pooled = (jnp.sum(stream[...], axis=0, keepdims=True) * (1.0 / tokens)).astype(BF16)
    w_head = w_head_ref[...].astype(BF16)
    pooled_rows = jnp.broadcast_to(pooled.astype(F32), (16, dim)).astype(BF16)
    logits = dot(pooled_rows, w_head, NN)
    peak = jnp.max(logits, axis=-1, keepdims=True)
    expd = jnp.exp(logits - peak)
    probs = expd / jnp.sum(expd, axis=-1, keepdims=True)
    class_ids = lax.broadcasted_iota(jnp.int32, logits.shape, 1)
    targets = jnp.where(class_ids == label_ref[0], 1.0, 0.0)
    d_logits = ((probs - targets) * (1.0 / n_shards)).astype(BF16)
    d_pooled = dot(d_logits, w_head, NT).astype(BF16).astype(F32) / tokens
    d_stream[...] = jnp.broadcast_to(d_pooled[0:1], d_stream.shape)
    head_send[...] = jnp.zeros_like(head_send)
    d_logits = d_logits.astype(F32)
    for chunk in range(8):
        wide = min(LANES, classes - chunk * LANES)
        head_send[chunk:chunk + 1, 0:wide] = d_logits[0:1, chunk * LANES:chunk * LANES + wide]
    pooled = pooled.astype(F32)
    head_send[8:9, :] = pooled[:, 0:LANES]
    head_send[9:10, 0:dim - LANES] = pooled[:, LANES:dim]
    head_recv[0] = head_send[...]

    pl.semaphore_wait(barrier, n_shards - 1)

    def head_copy(step):
        other = (me + step) % n_shards
        return pltpu.make_async_remote_copy(
            src_ref=head_send, dst_ref=head_recv.at[step], send_sem=head_send_sem.at[step],
            recv_sem=head_recv_sem.at[step], device_id=(other // 2, other % 2), device_id_type=MESH)

    for step in range(1, n_shards):
        head_copy(step).start()

    mine = half * core
    place_a, place_b = mine, mine + half // 2

    def remote(src, dst, layer, sem, device):
        return pltpu.make_async_remote_copy(
            src_ref=src, dst_ref=dst, send_sem=send_sem.at[layer, sem], recv_sem=recv_sem.at[layer, sem],
            device_id=device, device_id_type=MESH)

    def copies(stage, layer):
        def grad(start, size):
            return grads.at[layer, pl.ds(start, size)]

        def total(start, size):
            return sums.at[layer, pl.ds(start, size)]

        if stage == 0:
            return [remote(grad(half * (1 - core), half), recv0.at[layer], layer, 0, peer_core)]
        if stage == 1:
            return [remote(grad(place_a + quarter * (1 - x), quarter), recv1.at[layer, 0], layer, 1, peer_x),
                    remote(grad(place_b + quarter * (1 - y), quarter), recv1.at[layer, 1], layer, 2, peer_y)]
        if stage == 2:
            return [remote(grad(place_a + quarter * x + eighth * (1 - y), eighth), recv2.at[layer, 0], layer, 3, peer_y),
                    remote(grad(place_b + quarter * y + eighth * (1 - x), eighth), recv2.at[layer, 1], layer, 4, peer_x)]
        if stage == 3:
            spot_a = total(place_a + quarter * x + eighth * y, eighth)
            spot_b = total(place_b + quarter * y + eighth * x, eighth)
            return [remote(spot_a, spot_a, layer, 5, peer_y), remote(spot_b, spot_b, layer, 6, peer_x)]
        if stage == 4:
            spot_a = total(place_a + quarter * x, quarter)
            spot_b = total(place_b + quarter * y, quarter)
            return [remote(spot_a, spot_a, layer, 7, peer_x), remote(spot_b, spot_b, layer, 8, peer_y)]
        spot = total(mine, half)
        return [remote(spot, spot, layer, 9, peer_core)]

    def add(layer, dst, start, size, other):
        dst[layer, pl.ds(start, size)] = (
            grads[layer, pl.ds(start, size)].astype(F32) + other[...].astype(F32)).astype(BF16)

    def start(stage, layer):
        for copy in copies(stage, layer):
            copy.start()

    def finish(stage, layer):
        for copy in copies(stage, layer):
            copy.wait_recv()
        if stage == 0:
            add(layer, grads, mine, half, recv0.at[layer])
        elif stage == 1:
            add(layer, grads, place_a + quarter * x, quarter, recv1.at[layer, 0])
            add(layer, grads, place_b + quarter * y, quarter, recv1.at[layer, 1])
        elif stage == 2:
            add(layer, sums, place_a + quarter * x + eighth * y, eighth, recv2.at[layer, 0])
            add(layer, sums, place_b + quarter * y + eighth * x, eighth, recv2.at[layer, 1])

    def store(layer):
        return pltpu.make_async_copy(sums.at[layer], sums_hbm.at[layer], store_sem.at[layer])

    last_stage = 5

    def tick(turn):
        for stage in range(last_stage, -1, -1):
            source = turn - 1 - stage

            @pl.when((source >= 0) & (source < layers))
            def _():
                layer = layers - 1 - source
                finish(stage, layer)
                if stage < last_stage:
                    start(stage + 1, layer)
                else:
                    store(layer).start()

    def backward(turn, carry):
        layer = layers - 1 - turn
        for begin in range(0, tokens, rows):
            part = slice(begin, begin + rows)
            branch = d_stream[part].astype(BF16)
            d_branch[part] = branch
            d_hidden = dot(branch, w_out[layer], NN).astype(BF16).astype(F32)
            d_pre_part = (d_hidden * d_gelu[layer, part]).astype(BF16)
            d_pre[part] = d_pre_part
            d_act = dot(d_pre_part, w_in[layer], NT).astype(BF16).astype(F32)
            normed = x_hat[layer, part]
            mean_d = jnp.mean(d_act, axis=-1, keepdims=True)
            mean_dx = jnp.mean(d_act * normed, axis=-1, keepdims=True)
            d_stream[part] = d_stream[part] + rstds[layer, part] * (d_act - mean_d - normed * mean_dx)
        g_in = dot(acts[layer], d_pre[...], TN).astype(BF16)
        g_out = dot(d_branch[...], hidden[layer], TN).astype(BF16)
        for chunk in range(chunks):
            grads[layer, chunk * dim:(chunk + 1) * dim] = g_in[:, chunk * LANES:(chunk + 1) * LANES]
            grads[layer, half + chunk * dim:half + (chunk + 1) * dim] = g_out[:, chunk * LANES:(chunk + 1) * LANES]
        tick(turn)
        start(0, layer)
        return carry

    lax.fori_loop(0, layers, backward, 0)

    for step in range(1, n_shards):
        head_copy(step).wait_recv()
    columns = []
    for device in range(n_shards):
        turned = head_recv[device, 8:16, :].T
        columns.append(jnp.concatenate([turned[:, 0:1], turned[0:dim - LANES, 1:2]], axis=0))
    for chunk in range(8):
        wide = min(LANES, classes - chunk * LANES)
        total_head = None
        for device in range(n_shards):
            product = columns[device] * head_recv[device, chunk:chunk + 1, 0:wide]
            product = product.astype(BF16).astype(F32)
            total_head = product if total_head is None else total_head + product
        head_sum_ref[:, chunk * LANES:chunk * LANES + wide] = total_head

    def drain(turn, carry):
        tick(turn)
        return carry

    lax.fori_loop(layers, layers + last_stage + 1, drain, 0)

    def finish_all(layer, carry):
        for stage in range(last_stage + 1):
            for copy in copies(stage, layer):
                copy.wait_send()
        store(layer).wait()
        return carry

    lax.fori_loop(0, layers, finish_all, 0)
    for step in range(1, n_shards):
        head_copy(step).wait_send()


def update_kernel(rows, x_ref, rate_ref, w_in_ref, m_in_ref, w_out_ref, m_out_ref, sums_ref,
                  w_head_ref, m_head_ref, head_sum_ref,
                  logits_ref, w_in_new, m_in_new, w_out_new, m_out_new, w_head_new, m_head_new,
                  stream, w_in, w_out):
    layer, layers = pl.program_id(0), pl.num_programs(0)
    dim, tokens = x_ref.shape[1:]
    chunks = w_in.shape[1] // LANES
    half = chunks * dim
    rate, coef = rate_ref[0], rate_ref[1]

    @pl.when(layer == 0)
    def _():
        stream[...] = x_ref[0].astype(F32).T

    for chunk in range(chunks):
        columns = slice(chunk * LANES, (chunk + 1) * LANES)
        for base, w_ref, m_ref, w_new, m_new, w_bf in (
                (0, w_in_ref, m_in_ref, w_in_new, m_in_new, w_in),
                (half, w_out_ref, m_out_ref, w_out_new, m_out_new, w_out)):
            grad = sums_ref[0, base + chunk * dim:base + (chunk + 1) * dim].astype(F32)
            moment = coef * m_ref[0, :, columns] + grad
            m_new[0, :, columns] = moment
            weight = w_ref[0, :, columns] - rate * moment
            w_new[0, :, columns] = weight
            w_bf[:, columns] = weight.astype(BF16)

    for start in range(0, tokens, rows):
        part = slice(start, start + rows)
        stream_in = stream[part]
        act = normalize(stream_in)[0].astype(BF16)
        pre = dot(act, w_in[...], NN)
        tanh_val = jnp.tanh(pre * (GELU_SCALE + (GELU_SCALE * GELU_CUBIC) * (pre * pre)))
        out = (pre * (0.5 + 0.5 * tanh_val)).astype(BF16)
        stream[part] = stream_in + dot(out, w_out[...], NT)

    @pl.when(layer == layers - 1)
    def _():
        moment = coef * m_head_ref[...] + head_sum_ref[...]
        m_head_new[...] = moment
        weight = w_head_ref[...] - rate * moment
        w_head_new[...] = weight
        pooled = jnp.sum(stream[...], axis=0, keepdims=True) * (1.0 / tokens)
        pooled = jnp.broadcast_to(pooled, (16, dim)).astype(BF16)
        logits_ref[...] = dot(pooled, weight.astype(BF16), NN)[0:1]


def solution(mesh):
    batch_spec = P(BATCH_AXES)
    repl_spec = P()
    n_shards = mesh.shape["inner"] * mesh.shape["data"]

    def device_step(x_t, labels_t, x_next, w_in, w_out, w_head, mom_in, mom_out, mom_head, learn_rate, mom_coef):
        layers, dim, mlp_dim = w_in.shape
        tokens = x_t.shape[1]
        classes = w_head.shape[1]
        w_out_t = w_out.transpose(0, 2, 1)
        mom_out_t = mom_out.transpose(0, 2, 1)
        weight_rows = mlp_dim // LANES * dim
        vmem = pl.BlockSpec(memory_space=pltpu.VMEM)
        smem = pl.BlockSpec(memory_space=pltpu.SMEM)
        hbm = pl.BlockSpec(memory_space=pl.ANY)
        sums, head_sum = pl.pallas_call(
            functools.partial(step_kernel, n_shards, 192),
            out_shape=(jax.ShapeDtypeStruct((layers, 2 * weight_rows, LANES), BF16),
                       jax.ShapeDtypeStruct((dim, classes), F32)),
            in_specs=[vmem, smem, hbm, hbm, vmem],
            out_specs=(hbm, vmem),
            scratch_shapes=[
                pltpu.VMEM((tokens, dim), F32),
                pltpu.VMEM((tokens, dim), F32),
                pltpu.VMEM((layers, tokens, dim), F32),
                pltpu.VMEM((layers, tokens, 1), F32),
                pltpu.VMEM((layers, tokens, dim), BF16),
                pltpu.VMEM((layers, tokens, mlp_dim), BF16),
                pltpu.VMEM((layers, tokens, mlp_dim), F32),
                pltpu.VMEM((tokens, dim), BF16),
                pltpu.VMEM((tokens, mlp_dim), BF16),
                pltpu.VMEM((2, dim, mlp_dim), F32),
                pltpu.VMEM((2, dim, mlp_dim), F32),
                pltpu.VMEM((layers, dim, mlp_dim), BF16),
                pltpu.VMEM((layers, dim, mlp_dim), BF16),
                pltpu.VMEM((layers, 2 * weight_rows, LANES), BF16),
                pltpu.VMEM((layers, weight_rows, LANES), BF16),
                pltpu.VMEM((layers, 2, weight_rows // 4, LANES), BF16),
                pltpu.VMEM((layers, 2, weight_rows // 8, LANES), BF16),
                pltpu.VMEM((layers, 2 * weight_rows, LANES), BF16),
                pltpu.VMEM((16, LANES), F32),
                pltpu.VMEM((n_shards, 16, LANES), F32),
                pltpu.SemaphoreType.DMA((2, 2)),
                pltpu.SemaphoreType.DMA((layers,)),
                pltpu.SemaphoreType.DMA((layers, 10)),
                pltpu.SemaphoreType.DMA((layers, 10)),
                pltpu.SemaphoreType.DMA((n_shards,)),
                pltpu.SemaphoreType.DMA((n_shards,)),
            ],
            compiler_params=pltpu.CompilerParams(collective_id=0, has_side_effects=True, vmem_limit_bytes=VMEM_BYTES),
            name="step_kernel",
        )(x_t.transpose(0, 2, 1), labels_t, w_in, w_out_t, w_head)

        def per_layer(shape):
            return pl.BlockSpec((1,) + shape, lambda l: (l, 0, 0))

        def whole(shape):
            return pl.BlockSpec(shape, lambda l: (0,) * len(shape))

        weight_block = per_layer((dim, mlp_dim))
        head_block = whole((dim, classes))
        stacked = jax.ShapeDtypeStruct((layers, dim, mlp_dim), F32)
        head_shape = jax.ShapeDtypeStruct((dim, classes), F32)
        rates = jnp.stack([learn_rate, mom_coef])
        logits, w_in_new, m_in_new, w_out_new, m_out_new, w_head_new, m_head_new = pl.pallas_call(
            functools.partial(update_kernel, 192),
            grid=(layers,),
            out_shape=(jax.ShapeDtypeStruct((1, classes), F32), stacked, stacked, stacked, stacked, head_shape, head_shape),
            in_specs=[whole((1, dim, tokens)), smem, weight_block, weight_block, weight_block, weight_block,
                      per_layer((2 * weight_rows, LANES)), head_block, head_block, head_block],
            out_specs=(whole((1, classes)), weight_block, weight_block, weight_block, weight_block, head_block, head_block),
            scratch_shapes=[
                pltpu.VMEM((tokens, dim), F32),
                pltpu.VMEM((dim, mlp_dim), BF16),
                pltpu.VMEM((dim, mlp_dim), BF16),
            ],
            compiler_params=pltpu.CompilerParams(vmem_limit_bytes=VMEM_BYTES),
            name="update_kernel",
        )(x_next.transpose(0, 2, 1), rates, w_in, mom_in, w_out_t, mom_out_t, sums, w_head, mom_head, head_sum)
        return (logits, w_in_new, w_out_new.transpose(0, 2, 1), w_head_new,
                m_in_new, m_out_new.transpose(0, 2, 1), m_head_new)

    return jax.shard_map(device_step, mesh=mesh, in_specs=(batch_spec, batch_spec, batch_spec) + (repl_spec,) * 8, out_specs=(batch_spec,) + (repl_spec,) * 6, check_vma=False)
```

time: 672 us -> 96.5 us (0.14); the launches traced: 661 us -> 95.9 us
  waiting for transfers between devices: 299 us -> 0 us
  blocking collectives: 156 us -> 0 us
  matrix products: 104 us -> 0 us
  Pallas kernels: 0 us -> 92.7 us
  local copies, waits for them, and re-layouts: 47.1 us -> 0 us
  other arithmetic: 34.5 us -> 0.6 us
  between operations: 18.2 us -> 2.58 us
    reduce_scatter x17 -> x0, waiting for transfers between devices: 293 us -> none  [reduce_grad(): lax.psum_scatter(wire_grad, 'inner', scatter_dimension=0, tiled=True)]
    all_gather x17 -> x0, blocking collectives: 156 us -> none  [reduce_grad(): lax.all_gather(grad_shard, 'inner', axis=0, tiled=True).astype(jnp.float32)]
    dot_general x57 -> x0, matrix products: 104 us -> none  [the longest x7 21 us: local_backward(): jnp.einsum('bsd,fd->bsf', d_branch, out_bf[layer_idx], preferred_element_...]
    pallas_call x0 -> x2, Pallas kernels: none -> 92.7 us  [the longest x1 70.7 us: device_step(): pl.pallas_call(functools.partial(step_kernel, n_shards, 192), out_shape=(...]
    unnamed x176 -> x0, local copies, waits for them, and re-layouts: 47.1 us -> none
    convert_element_type x8 -> x0, other arithmetic: 25.2 us -> none  [the longest x1 11.8 us: device_step(): new_w_out.astype(jnp.bfloat16)]
  transfers between devices with their start and end apart: 18 -> 0, of which waited for: 15 -> 0; matrix products, arithmetic and copies ran while one was open for 11% -> 0% of each run, Pallas kernels for 0% -> 0%
where the time goes in v1:
time: 96.5 us; the launch traced here: 95.9 us
  Pallas kernels  92.7 us (96%)
  between operations  2.58 us (3%)
    pallas_call x1, Pallas kernels, device_step(): pl.pallas_call(functools.partial(step_kernel, n_shards, 192), out_shape=(...  70.7 us
    pallas_call x1, Pallas kernels, device_step(): pl.pallas_call(functools.partial(update_kernel, 192), grid=(layers,), out...  22 us

profile of v1, /device:TPU:0, one launch (start us, length us, event | category | flops | bytes accessed | tf_op | source)
XLA Modules:
  0.0 95.9 jit_solution(1140263620334931426)
XLA Ops:
  2.6 0.6 pad_maximum_fusion.rate_ref
  3.2 70.7 %step_kernel.1 = (bf16[8,2304,128]{2,1,0:T(8,128)(2,1)}, f32[192,1000]{1,0:T(8,128)}) custom-call(bf16[1,192,576]{2,1,0:T(8,128)(2,1)} %bitcast.14, s32[1]{0:T(128)S(6)} %copy.18.label_ref, f32[8,192,768]{2,1,0:T(8,128)} %w_in_ref.1, f32[8,192,768]{2,1,0:T(8,128)} %bitcast.10, f32[192,1000]{1,0:T(8,128)} %w_head_ref.3), custom_call_target="tpu_custom_call" | custom-call | tf_op jit(solution)/shard_map/step_kernel/pallas_call | solution.py:326
  73.9 22.0 %update_kernel.1 = (f32[1,1000]{1,0:T(1,128)}, f32[8,192,768]{2,1,0:T(8,128)}, f32[8,192,768]{2,1,0:T(8,128)}, f32[8,192,768]{2,1,0:T(8,128)}, f32[8,192,768]{2,...) custom-call(bf16[1,192,576]{2,1,0:T(8,128)(2,1)} %bitcast.13, f32[2]{0:T(128)} %pad_maximum_fusion.rate_ref, ...), custom_call_target="tpu_custom_call" | custom-call | tf_op jit(solution)/shard_map/update_kernel/pallas_call | solution.py:375

commit v2 on v1

v2 whole, which is shorter than its diff:
```python
import functools

import jax
import jax.numpy as jnp
from jax import lax
from jax.experimental import pallas as pl
from jax.experimental.pallas import tpu as pltpu
from jax.sharding import PartitionSpec as P

LN_EPS = 1e-6
BATCH_AXES = ("inner", "data")
MESH = pl.DeviceIdType.MESH
LANES = 128
GELU_SCALE = 0.7978845608028654
GELU_CUBIC = 0.044715
F32 = jnp.float32
BF16 = jnp.bfloat16
NT = (((1,), (1,)), ((), ()))
NN = (((1,), (0,)), ((), ()))
TN = (((0,), (0,)), ((), ()))
VMEM_BYTES = 45 * 1000 * 1000
ROWS = 192


def dot(a, b, dims):
    return lax.dot_general(a, b, dims, preferred_element_type=F32)


def normalize(stream):
    mean_val = jnp.mean(stream, axis=-1, keepdims=True)
    centered = stream - mean_val
    variance = jnp.mean(centered * centered, axis=-1, keepdims=True)
    rstd = lax.rsqrt(variance + LN_EPS)
    return centered * rstd, rstd


def gelu_parts(pre):
    inner = GELU_SCALE + (GELU_SCALE * GELU_CUBIC) * (pre * pre)
    return inner, 0.5 + 0.5 * jnp.tanh(pre * inner)


def step_kernel(n_shards,
                x_ref, x_next_ref, label_ref, rate_ref, coef_ref, w_in_hbm, w_out_hbm, w_head_hbm, m_in_hbm, m_out_hbm, m_head_hbm,
                w_in_ref, w_out_ref, w_head_ref, m_in_ref, m_out_ref, m_head_ref, logits_ref,
                stream, d_stream, x_hat, acts, hidden, d_branch, d_pre, w_in, w_out,
                grads, recv0, recv1, recv2, sums, head_send, head_recv,
                load_sem, mom_sem, send_sem, recv_sem, head_send_sem, head_recv_sem):
    layers, tokens, mlp_dim = hidden.shape
    dim = stream.shape[1]
    classes = w_head_ref.shape[1]
    chunks = mlp_dim // LANES
    half = chunks * dim
    quarter, eighth = half // 4, half // 8
    parts = [slice(start, start + ROWS) for start in range(0, tokens, ROWS)]
    inner, core = lax.axis_index("inner"), lax.axis_index("data")
    y, x = inner // 2, inner % 2
    peer_core = (inner, 1 - core)
    peer_x = (inner + 1 - 2 * x, core)
    peer_y = (inner + 2 - 4 * y, core)
    barrier = pltpu.get_barrier_semaphore()
    me = inner * 2 + core

    def load(layer):
        return (pltpu.make_async_copy(w_in_hbm.at[layer], w_in_ref.at[layer], load_sem.at[layer, 0]),
                pltpu.make_async_copy(w_out_hbm.at[layer], w_out_ref.at[layer], load_sem.at[layer, 1]))

    mom_loads = (pltpu.make_async_copy(w_head_hbm, w_head_ref, mom_sem.at[0]),
                 pltpu.make_async_copy(m_head_hbm, m_head_ref, mom_sem.at[1]),
                 pltpu.make_async_copy(m_in_hbm, m_in_ref, mom_sem.at[2]),
                 pltpu.make_async_copy(m_out_hbm, m_out_ref, mom_sem.at[3]))

    for copy in load(0) + load(1):
        copy.start()
    for step in range(1, n_shards):
        other = (me + step) % n_shards
        pl.semaphore_signal(barrier, inc=1, device_id=(other // 2, other % 2), device_id_type=MESH)
    stream[...] = x_ref[0].astype(F32).T

    def forward(layer, carry):
        @pl.when(layer + 2 < layers)
        def _():
            for copy in load(layer + 2):
                copy.start()

        @pl.when(layer == layers - 2)
        def _():
            for copy in mom_loads:
                copy.start()

        for copy in load(layer):
            copy.wait()
        w_in[layer] = w_in_ref[layer].astype(BF16)
        w_out[layer] = w_out_ref[layer].astype(BF16)
        for part in parts:
            stream_in = stream[part]
            normed, rstd = normalize(stream_in)
            x_hat[layer, part, 0:dim] = normed
            x_hat[layer, part, dim:dim + 1] = rstd
            pre = dot(normed.astype(BF16), w_in[layer], NN)
            out = (pre * gelu_parts(pre)[1]).astype(BF16)
            hidden[layer, part] = out
            stream[part] = stream_in + dot(out, w_out[layer], NT)
        return carry

    lax.fori_loop(0, layers, forward, 0)

    pooled = (jnp.sum(stream[...], axis=0, keepdims=True) * (1.0 / tokens)).astype(BF16)
    mom_loads[0].wait()
    w_head = w_head_ref[...].astype(BF16)
    pooled_rows = jnp.broadcast_to(pooled.astype(F32), (16, dim)).astype(BF16)
    logits = dot(pooled_rows, w_head, NN)
    peak = jnp.max(logits, axis=-1, keepdims=True)
    expd = jnp.exp(logits - peak)
    probs = expd / jnp.sum(expd, axis=-1, keepdims=True)
    class_ids = lax.broadcasted_iota(jnp.int32, logits.shape, 1)
    targets = jnp.where(class_ids == label_ref[0], 1.0, 0.0)
    d_logits = ((probs - targets) * (1.0 / n_shards)).astype(BF16)
    d_pooled = dot(d_logits, w_head, NT).astype(BF16).astype(F32) / tokens
    d_stream[...] = jnp.broadcast_to(d_pooled[0:1], d_stream.shape)
    head_send[...] = jnp.zeros_like(head_send)
    d_logits = d_logits.astype(F32)
    for chunk in range(8):
        wide = min(LANES, classes - chunk * LANES)
        head_send[chunk:chunk + 1, 0:wide] = d_logits[0:1, chunk * LANES:chunk * LANES + wide]
    pooled = pooled.astype(F32)
    head_send[8:9, :] = pooled[:, 0:LANES]
    head_send[9:10, 0:dim - LANES] = pooled[:, LANES:dim]
    head_recv[0] = head_send[...]

    pl.semaphore_wait(barrier, n_shards - 1)

    def head_copy(step):
        other = (me + step) % n_shards
        return pltpu.make_async_remote_copy(
            src_ref=head_send, dst_ref=head_recv.at[step], send_sem=head_send_sem.at[step],
            recv_sem=head_recv_sem.at[step], device_id=(other // 2, other % 2), device_id_type=MESH)

    for step in range(1, n_shards):
        head_copy(step).start()

    mine = half * core
    place_a, place_b = mine, mine + half // 2

    def remote(src, dst, layer, sem, device):
        return pltpu.make_async_remote_copy(
            src_ref=src, dst_ref=dst, send_sem=send_sem.at[layer, sem], recv_sem=recv_sem.at[layer, sem],
            device_id=device, device_id_type=MESH)

    def copies(stage, layer):
        def grad(start, size):
            return grads.at[layer, pl.ds(start, size)]

        def total(start, size):
            return sums.at[layer, pl.ds(start, size)]

        if stage == 0:
            return [remote(grad(half * (1 - core), half), recv0.at[layer], layer, 0, peer_core)]
        if stage == 1:
            return [remote(grad(place_a + quarter * (1 - x), quarter), recv1.at[layer, 0], layer, 1, peer_x),
                    remote(grad(place_b + quarter * (1 - y), quarter), recv1.at[layer, 1], layer, 2, peer_y)]
        if stage == 2:
            return [remote(grad(place_a + quarter * x + eighth * (1 - y), eighth), recv2.at[layer, 0], layer, 3, peer_y),
                    remote(grad(place_b + quarter * y + eighth * (1 - x), eighth), recv2.at[layer, 1], layer, 4, peer_x)]
        if stage == 3:
            spot_a = total(place_a + quarter * x + eighth * y, eighth)
            spot_b = total(place_b + quarter * y + eighth * x, eighth)
            return [remote(spot_a, spot_a, layer, 5, peer_y), remote(spot_b, spot_b, layer, 6, peer_x)]
        if stage == 4:
            spot_a = total(place_a + quarter * x, quarter)
            spot_b = total(place_b + quarter * y, quarter)
            return [remote(spot_a, spot_a, layer, 7, peer_x), remote(spot_b, spot_b, layer, 8, peer_y)]
        spot = total(mine, half)
        return [remote(spot, spot, layer, 9, peer_core)]

    def add(layer, dst, start, size, other):
        dst[layer, pl.ds(start, size)] = (
            grads[layer, pl.ds(start, size)].astype(F32) + other[...].astype(F32)).astype(BF16)

    def start(stage, turn):
        for copy in copies(stage, layers - 1 - turn):
            copy.start()

    def advance(stage, turn):
        layer = layers - 1 - turn
        for copy in copies(stage, layer):
            copy.wait_recv()
        if stage == 0:
            add(layer, grads, mine, half, recv0.at[layer])
        elif stage == 1:
            add(layer, grads, place_a + quarter * x, quarter, recv1.at[layer, 0])
            add(layer, grads, place_b + quarter * y, quarter, recv1.at[layer, 1])
        elif stage == 2:
            add(layer, sums, place_a + quarter * x + eighth * y, eighth, recv2.at[layer, 0])
            add(layer, sums, place_b + quarter * y + eighth * x, eighth, recv2.at[layer, 1])
        if stage < 5:
            start(stage + 1, turn)

    def backward(turn, carry):
        layer = layers - 1 - turn
        for part in parts:
            branch = d_stream[part].astype(BF16)
            d_branch[part] = branch
            normed = x_hat[layer, part, 0:dim]
            act = normed.astype(BF16)
            acts[part] = act
            pre = dot(act, w_in[layer], NN)
            inner_val, cdf = gelu_parts(pre)
            slope = cdf + ((cdf - cdf * cdf) * pre) * (6.0 * inner_val - 4.0 * GELU_SCALE)
            d_hidden = dot(branch, w_out[layer], NN).astype(BF16).astype(F32)
            d_pre_part = (d_hidden * slope).astype(BF16)
            d_pre[part] = d_pre_part
            d_act = dot(d_pre_part, w_in[layer], NT).astype(BF16).astype(F32)
            mean_d = jnp.mean(d_act, axis=-1, keepdims=True)
            mean_dx = jnp.mean(d_act * normed, axis=-1, keepdims=True)
            d_stream[part] = d_stream[part] + x_hat[layer, part, dim:dim + 1] * (d_act - mean_d - normed * mean_dx)
        g_in = dot(acts[...], d_pre[...], TN).astype(BF16)
        g_out = dot(d_branch[...], hidden[layer], TN).astype(BF16)
        for chunk in range(chunks):
            grads[layer, chunk * dim:(chunk + 1) * dim] = g_in[:, chunk * LANES:(chunk + 1) * LANES]
            grads[layer, half + chunk * dim:half + (chunk + 1) * dim] = g_out[:, chunk * LANES:(chunk + 1) * LANES]
        start(0, turn)
        pl.when(turn >= 1)(lambda: advance(0, turn - 1))
        pl.when(turn >= 3)(lambda: advance(1, turn - 3))
        return carry

    lax.fori_loop(0, layers, backward, 0)
    last = layers - 1
    advance(0, last)
    advance(1, last - 2)

    rate, coef = rate_ref[0], coef_ref[0]
    for step in range(1, n_shards):
        head_copy(step).wait_recv()
    for copy in mom_loads[1:]:
        copy.wait()
    columns = []
    for device in range(n_shards):
        turned = head_recv[device, 8:16, :].T
        columns.append(jnp.concatenate([turned[:, 0:1], turned[0:dim - LANES, 1:2]], axis=0))
    for chunk in range(8):
        wide = min(LANES, classes - chunk * LANES)
        lanes = slice(chunk * LANES, chunk * LANES + wide)
        total_head = None
        for device in range(n_shards):
            product = columns[device] * head_recv[device, chunk:chunk + 1, 0:wide]
            product = product.astype(BF16).astype(F32)
            total_head = product if total_head is None else total_head + product
        moment = coef * m_head_ref[:, lanes] + total_head
        m_head_ref[:, lanes] = moment
        w_head_ref[:, lanes] = w_head_ref[:, lanes] - rate * moment
    stream[...] = x_next_ref[0].astype(F32).T

    for stage, turn in ((2, 0), (2, 1), (1, last - 1), (2, 2), (2, 3), (1, last), (2, 4), (2, 5), (2, last - 1),
                        (3, 0), (2, last), (3, 1), (3, last), (3, last - 1), (3, 5), (3, 4), (3, 3), (3, 2), (4, last)):
        advance(stage, turn)

    def next_forward(layer, carry):
        advance(5, last - layer)
        for chunk in range(chunks):
            lanes = slice(chunk * LANES, (chunk + 1) * LANES)
            for base, w_ref, m_ref, w_bf in ((0, w_in_ref, m_in_ref, w_in), (half, w_out_ref, m_out_ref, w_out)):
                grad = sums[layer, base + chunk * dim:base + (chunk + 1) * dim].astype(F32)
                moment = coef * m_ref[layer, :, lanes] + grad
                m_ref[layer, :, lanes] = moment
                weight = w_ref[layer, :, lanes] - rate * moment
                w_ref[layer, :, lanes] = weight
                w_bf[layer, :, lanes] = weight.astype(BF16)
        pl.when(layer < last)(lambda: advance(4, last - 1 - layer))
        for part in parts:
            stream_in = stream[part]
            pre = dot(normalize(stream_in)[0].astype(BF16), w_in[layer], NN)
            out = (pre * gelu_parts(pre)[1]).astype(BF16)
            stream[part] = stream_in + dot(out, w_out[layer], NT)
        return carry

    lax.fori_loop(0, layers, next_forward, 0)
    pooled = jnp.sum(stream[...], axis=0, keepdims=True) * (1.0 / tokens)
    pooled = jnp.broadcast_to(pooled, (16, dim)).astype(BF16)
    logits_ref[...] = dot(pooled, w_head_ref[...].astype(BF16), NN)[0:1]

    def finish_all(layer, carry):
        for stage in range(6):
            for copy in copies(stage, layer):
                copy.wait_send()
        return carry

    lax.fori_loop(0, layers, finish_all, 0)
    for step in range(1, n_shards):
        head_copy(step).wait_send()


def store_kernel(*refs):
    count = (len(refs) - 1) // 2
    copies = [pltpu.make_async_copy(refs[i], refs[count + i], refs[-1].at[i]) for i in range(count)]
    for copy in copies:
        copy.start()
    for copy in copies:
        copy.wait()


def solution(mesh):
    batch_spec = P(BATCH_AXES)
    repl_spec = P()
    n_shards = mesh.shape["inner"] * mesh.shape["data"]

    def device_step(x_t, labels_t, x_next, w_in, w_out, w_head, mom_in, mom_out, mom_head, learn_rate, mom_coef):
        layers, dim, mlp_dim = w_in.shape
        tokens = x_t.shape[1]
        classes = w_head.shape[1]
        half = mlp_dim // LANES * dim
        vmem = pl.BlockSpec(memory_space=pltpu.VMEM)
        smem = pl.BlockSpec(memory_space=pltpu.SMEM)
        hbm = pl.BlockSpec(memory_space=pl.ANY)
        shapes = [(layers, dim, mlp_dim), (layers, dim, mlp_dim), (dim, classes)] * 2 + [(1, classes)]
        results = pl.pallas_call(
            functools.partial(step_kernel, n_shards),
            out_shape=tuple(pltpu.VMEM(shape, F32) for shape in shapes),
            in_specs=[vmem, vmem, smem, smem, smem] + [hbm] * 6,
            out_specs=(vmem,) * 7,
            scratch_shapes=[
                pltpu.VMEM((tokens, dim), F32),
                pltpu.VMEM((tokens, dim), F32),
                pltpu.VMEM((layers, tokens, dim + 1), F32),
                pltpu.VMEM((tokens, dim), BF16),
                pltpu.VMEM((layers, tokens, mlp_dim), BF16),
                pltpu.VMEM((tokens, dim), BF16),
                pltpu.VMEM((tokens, mlp_dim), BF16),
                pltpu.VMEM((layers, dim, mlp_dim), BF16),
                pltpu.VMEM((layers, dim, mlp_dim), BF16),
                pltpu.VMEM((layers, 2 * half, LANES), BF16),
                pltpu.VMEM((layers, half, LANES), BF16),
                pltpu.VMEM((layers, 2, half // 4, LANES), BF16),
                pltpu.VMEM((layers, 2, half // 8, LANES), BF16),
                pltpu.VMEM((layers, 2 * half, LANES), BF16),
                pltpu.VMEM((16, LANES), F32),
                pltpu.VMEM((n_shards, 16, LANES), F32),
                pltpu.SemaphoreType.DMA((layers, 2)),
                pltpu.SemaphoreType.DMA((4,)),
                pltpu.SemaphoreType.DMA((layers, 10)),
                pltpu.SemaphoreType.DMA((layers, 10)),
                pltpu.SemaphoreType.DMA((n_shards,)),
                pltpu.SemaphoreType.DMA((n_shards,)),
            ],
            compiler_params=pltpu.CompilerParams(collective_id=0, has_side_effects=True, vmem_limit_bytes=VMEM_BYTES),
            name="step_kernel",
        )(x_t.transpose(0, 2, 1), x_next.transpose(0, 2, 1), labels_t, learn_rate.reshape(1), mom_coef.reshape(1),
          w_in, w_out.transpose(0, 2, 1), w_head, mom_in, mom_out.transpose(0, 2, 1), mom_head)
        stored = pl.pallas_call(
            store_kernel,
            out_shape=tuple(jax.ShapeDtypeStruct(shape, F32) for shape in shapes),
            in_specs=[vmem] * 7,
            out_specs=(hbm,) * 7,
            scratch_shapes=[pltpu.SemaphoreType.DMA((7,))],
            compiler_params=pltpu.CompilerParams(vmem_limit_bytes=1000 * 1000),
            name="store_kernel",
        )(*results)
        w_in_new, w_out_new, w_head_new, m_in_new, m_out_new, m_head_new, logits = stored
        return (logits, w_in_new, w_out_new.transpose(0, 2, 1), w_head_new,
                m_in_new, m_out_new.transpose(0, 2, 1), m_head_new)

    return jax.shard_map(device_step, mesh=mesh, in_specs=(batch_spec, batch_spec, batch_spec) + (repl_spec,) * 8, out_specs=(batch_spec,) + (repl_spec,) * 6, check_vma=False)
```

time: 96.5 us -> 79.5 us (0.82)
  Pallas kernels: 92.7 us -> 76.8 us
    pallas_call x2, Pallas kernels: 92.7 us -> 76.8 us  [the longest x1 69.8 us: device_step(): pl.pallas_call(functools.partial(step_kernel, n_shards), out_shape=tuple(...]
where the time goes in v2:
time: 79.5 us; the launch traced here: 79.4 us
  Pallas kernels  76.8 us (97%)
  between operations  2.58 us (3%)
    pallas_call x1, Pallas kernels, device_step(): pl.pallas_call(functools.partial(step_kernel, n_shards), out_shape=tuple(...  69.8 us
    pallas_call x1, Pallas kernels, device_step(): pl.pallas_call(store_kernel, out_shape=tuple((jax.ShapeDtypeStruct(shape,...  6.99 us

profile of v2, /device:TPU:0, one launch (start us, length us, event | category | flops | bytes accessed | tf_op | source)
XLA Modules:
  0.0 79.4 jit_solution(2379558809850726025)
XLA Ops:
  2.6 69.8 %step_kernel.1 = (f32[8,192,768]{2,1,0:T(8,128)S(1)}, f32[8,192,768]{2,1,0:T(8,128)S(1)}, f32[192,1000]{1,0:T(8,128)S(1)}, f32[8,192,768]{2,1,0:T(8,128)S(1)}, f...) custom-call(bf16[1,192,576]{2,1,0:T(8,128)(2,1)} %bitcast.12, ...), custom_call_target="tpu_custom_call" | custom-call | tf_op jit(solution)/shard_map/step_kernel/pallas_call | solution.py:315
  72.4 7.0 %store_kernel.1 = (f32[8,192,768]{2,1,0:T(8,128)}, f32[8,192,768]{2,1,0:T(8,128)}, f32[192,1000]{1,0:T(8,128)}, f32[8,192,768]{2,1,0:T(8,128)}, f32[8,192,768]{2...) custom-call(f32[8,192,768]{2,1,0:T(8,128)S(1)} %get-tuple-element.21.refs_0_, ...), custom_call_target="tpu_custom_call" | custom-call | tf_op jit(solution)/shard_map/store_kernel/pallas_call | solution.py:348

commit v3 on v2

--- a/solution.py
+++ b/solution.py
@@ -18,7 +18,7 @@
 NT = (((1,), (1,)), ((), ()))
 NN = (((1,), (0,)), ((), ()))
 TN = (((0,), (0,)), ((), ()))
-VMEM_BYTES = 45 * 1000 * 1000
+VMEM_BYTES = 46 * 1000 * 1000
 ROWS = 192
 
 
@@ -39,13 +39,20 @@
     return inner, 0.5 + 0.5 * jnp.tanh(pre * inner)
 
 
+AFTER_BACKWARD = [[], [(0, 0)], [(0, 1)], [(0, 2)], [(1, 0), (0, 3)], [(1, 1), (0, 4)], [(0, 5)], []]
+BEFORE_HEAD = [(0, 6), (0, 7), (2, 1), (1, 5), (1, 4), (1, 6), (2, 0), (1, 7), (1, 3), (1, 2), (2, 5), (2, 6), (2, 7), (2, 4), (2, 3), (2, 2), (3, 5), (3, 7), (3, 6)]
+AFTER_HEAD = [(4, 5), (3, 4), (5, 5), (3, 3), (3, 2), (4, 7), (4, 6), (5, 7)]
+BEFORE_UPDATE = [[], [(5, 6)], [], [(5, 4), (4, 3)], [(4, 2), (5, 3)], [(5, 2), (4, 1)], [(4, 0), (5, 1)], [(5, 0)]]
+AFTER_UPDATE = [[(3, 1), (3, 0)], [(4, 4)], [], [], [], [], [], []]
+
+
 def step_kernel(n_shards,
                 x_ref, x_next_ref, label_ref, rate_ref, coef_ref, w_in_hbm, w_out_hbm, w_head_hbm, m_in_hbm, m_out_hbm, m_head_hbm,
                 w_in_ref, w_out_ref, w_head_ref, m_in_ref, m_out_ref, m_head_ref, logits_ref,
-                stream, d_stream, x_hat, acts, hidden, d_branch, d_pre, w_in, w_out,
+                stream, d_stream, x_hat, acts, pre_acts, hidden, d_branch, d_pre, w_in, w_out,
                 grads, recv0, recv1, recv2, sums, head_send, head_recv,
                 load_sem, mom_sem, send_sem, recv_sem, head_send_sem, head_recv_sem):
-    layers, tokens, mlp_dim = hidden.shape
+    layers, tokens, mlp_dim = pre_acts.shape
     dim = stream.shape[1]
     classes = w_head_ref.shape[1]
     chunks = mlp_dim // LANES
@@ -97,8 +104,8 @@
             x_hat[layer, part, 0:dim] = normed
             x_hat[layer, part, dim:dim + 1] = rstd
             pre = dot(normed.astype(BF16), w_in[layer], NN)
+            pre_acts[layer, part] = pre
             out = (pre * gelu_parts(pre)[1]).astype(BF16)
-            hidden[layer, part] = out
             stream[part] = stream_in + dot(out, w_out[layer], NT)
         return carry
 
@@ -195,16 +202,25 @@
         if stage < 5:
             start(stage + 1, turn)
 
+    def run(steps):
+        for step in steps:
+            advance(*step)
+
+    def run_at(index, table):
+        for at, steps in enumerate(table):
+            if steps:
+                pl.when(index == at)(functools.partial(run, steps))
+
     def backward(turn, carry):
         layer = layers - 1 - turn
         for part in parts:
             branch = d_stream[part].astype(BF16)
             d_branch[part] = branch
             normed = x_hat[layer, part, 0:dim]
-            act = normed.astype(BF16)
-            acts[part] = act
-            pre = dot(act, w_in[layer], NN)
+            acts[part] = normed.astype(BF16)
+            pre = pre_acts[layer, part]
             inner_val, cdf = gelu_parts(pre)
+            hidden[part] = (pre * cdf).astype(BF16)
             slope = cdf + ((cdf - cdf * cdf) * pre) * (6.0 * inner_val - 4.0 * GELU_SCALE)
             d_hidden = dot(branch, w_out[layer], NN).astype(BF16).astype(F32)
             d_pre_part = (d_hidden * slope).astype(BF16)
@@ -214,19 +230,17 @@
             mean_dx = jnp.mean(d_act * normed, axis=-1, keepdims=True)
             d_stream[part] = d_stream[part] + x_hat[layer, part, dim:dim + 1] * (d_act - mean_d - normed * mean_dx)
         g_in = dot(acts[...], d_pre[...], TN).astype(BF16)
-        g_out = dot(d_branch[...], hidden[layer], TN).astype(BF16)
+        g_out = dot(d_branch[...], hidden[...], TN).astype(BF16)
         for chunk in range(chunks):
             grads[layer, chunk * dim:(chunk + 1) * dim] = g_in[:, chunk * LANES:(chunk + 1) * LANES]
             grads[layer, half + chunk * dim:half + (chunk + 1) * dim] = g_out[:, chunk * LANES:(chunk + 1) * LANES]
         start(0, turn)
-        pl.when(turn >= 1)(lambda: advance(0, turn - 1))
-        pl.when(turn >= 3)(lambda: advance(1, turn - 3))
+        run_at(turn, AFTER_BACKWARD)
         return carry
 
     lax.fori_loop(0, layers, backward, 0)
     last = layers - 1
-    advance(0, last)
-    advance(1, last - 2)
+    run(BEFORE_HEAD)
 
     rate, coef = rate_ref[0], coef_ref[0]
     for step in range(1, n_shards):
@@ -250,12 +264,10 @@
         w_head_ref[:, lanes] = w_head_ref[:, lanes] - rate * moment
     stream[...] = x_next_ref[0].astype(F32).T
 
-    for stage, turn in ((2, 0), (2, 1), (1, last - 1), (2, 2), (2, 3), (1, last), (2, 4), (2, 5), (2, last - 1),
-                        (3, 0), (2, last), (3, 1), (3, last), (3, last - 1), (3, 5), (3, 4), (3, 3), (3, 2), (4, last)):
-        advance(stage, turn)
+    run(AFTER_HEAD)
 
     def next_forward(layer, carry):
-        advance(5, last - layer)
+        run_at(layer, BEFORE_UPDATE)
         for chunk in range(chunks):
             lanes = slice(chunk * LANES, (chunk + 1) * LANES)
             for base, w_ref, m_ref, w_bf in ((0, w_in_ref, m_in_ref, w_in), (half, w_out_ref, m_out_ref, w_out)):
@@ -265,7 +277,7 @@
                 weight = w_ref[layer, :, lanes] - rate * moment
                 w_ref[layer, :, lanes] = weight
                 w_bf[layer, :, lanes] = weight.astype(BF16)
-        pl.when(layer < last)(lambda: advance(4, last - 1 - layer))
+        run_at(layer, AFTER_UPDATE)
         for part in parts:
             stream_in = stream[part]
             pre = dot(normalize(stream_in)[0].astype(BF16), w_in[layer], NN)
@@ -322,7 +334,8 @@
                 pltpu.VMEM((tokens, dim), F32),
                 pltpu.VMEM((layers, tokens, dim + 1), F32),
                 pltpu.VMEM((tokens, dim), BF16),
-                pltpu.VMEM((layers, tokens, mlp_dim), BF16),
+                pltpu.VMEM((layers, tokens, mlp_dim), F32),
+                pltpu.VMEM((tokens, mlp_dim), BF16),
                 pltpu.VMEM((tokens, dim), BF16),
                 pltpu.VMEM((tokens, mlp_dim), BF16),
                 pltpu.VMEM((layers, dim, mlp_dim), BF16),

time: 79.5 us -> 73.9 us (0.930)
  Pallas kernels: 76.8 us -> 71.2 us
    pallas_call x1, Pallas kernels: 69.8 us -> 64.2 us  [device_step(): pl.pallas_call(functools.partial(step_kernel, n_shards), out_shape=tuple(...]
where the time goes in v3:
time: 73.9 us; the launch traced here: 73.8 us
  Pallas kernels  71.2 us (96%)
  between operations  2.58 us (3%)
    pallas_call x1, Pallas kernels, device_step(): pl.pallas_call(functools.partial(step_kernel, n_shards), out_shape=tuple(...  64.2 us
    pallas_call x1, Pallas kernels, device_step(): pl.pallas_call(store_kernel, out_shape=tuple((jax.ShapeDtypeStruct(shape,...  6.99 us

profile of v3, /device:TPU:0, one launch (start us, length us, event | category | flops | bytes accessed | tf_op | source)
XLA Modules:
  0.0 73.8 jit_solution(15195994677708858322)
XLA Ops:
  2.6 64.2 %step_kernel.1 = (f32[8,192,768]{2,1,0:T(8,128)S(1)}, f32[8,192,768]{2,1,0:T(8,128)S(1)}, f32[192,1000]{1,0:T(8,128)S(1)}, f32[8,192,768]{2,1,0:T(8,128)S(1)}, f...) custom-call(bf16[1,192,576]{2,1,0:T(8,128)(2,1)} %bitcast.12, ...), custom_call_target="tpu_custom_call" | custom-call | tf_op jit(solution)/shard_map/step_kernel/pallas_call | solution.py:327
  66.8 7.0 %store_kernel.1 = (f32[8,192,768]{2,1,0:T(8,128)}, f32[8,192,768]{2,1,0:T(8,128)}, f32[192,1000]{1,0:T(8,128)}, f32[8,192,768]{2,1,0:T(8,128)}, f32[8,192,768]{2...) custom-call(f32[8,192,768]{2,1,0:T(8,128)S(1)} %get-tuple-element.21.refs_0_, ...), custom_call_target="tpu_custom_call" | custom-call | tf_op jit(solution)/shard_map/store_kernel/pallas_call | solution.py:361

commit v4 on v3

--- a/solution.py
+++ b/solution.py
@@ -120,7 +120,7 @@
     expd = jnp.exp(logits - peak)
     probs = expd / jnp.sum(expd, axis=-1, keepdims=True)
     class_ids = lax.broadcasted_iota(jnp.int32, logits.shape, 1)
-    targets = jnp.where(class_ids == label_ref[0], 1.0, 0.0)
+    targets = jnp.where(class_ids == label_ref[...], 1.0, 0.0)
     d_logits = ((probs - targets) * (1.0 / n_shards)).astype(BF16)
     d_pooled = dot(d_logits, w_head, NT).astype(BF16).astype(F32) / tokens
     d_stream[...] = jnp.broadcast_to(d_pooled[0:1], d_stream.shape)
@@ -213,7 +213,7 @@
 
     def backward(turn, carry):
         layer = layers - 1 - turn
-        for part in parts:
+        for part in (slice(0, tokens),):
             branch = d_stream[part].astype(BF16)
             d_branch[part] = branch
             normed = x_hat[layer, part, 0:dim]
@@ -242,7 +242,7 @@
     last = layers - 1
     run(BEFORE_HEAD)
 
-    rate, coef = rate_ref[0], coef_ref[0]
+    rate, coef = rate_ref[...], coef_ref[...]
     for step in range(1, n_shards):
         head_copy(step).wait_recv()
     for copy in mom_loads[1:]:
@@ -321,13 +321,12 @@
         classes = w_head.shape[1]
         half = mlp_dim // LANES * dim
         vmem = pl.BlockSpec(memory_space=pltpu.VMEM)
-        smem = pl.BlockSpec(memory_space=pltpu.SMEM)
         hbm = pl.BlockSpec(memory_space=pl.ANY)
         shapes = [(layers, dim, mlp_dim), (layers, dim, mlp_dim), (dim, classes)] * 2 + [(1, classes)]
         results = pl.pallas_call(
             functools.partial(step_kernel, n_shards),
             out_shape=tuple(pltpu.VMEM(shape, F32) for shape in shapes),
-            in_specs=[vmem, vmem, smem, smem, smem] + [hbm] * 6,
+            in_specs=[vmem] * 5 + [hbm] * 6,
             out_specs=(vmem,) * 7,
             scratch_shapes=[
                 pltpu.VMEM((tokens, dim), F32),
@@ -356,7 +355,7 @@
             ],
             compiler_params=pltpu.CompilerParams(collective_id=0, has_side_effects=True, vmem_limit_bytes=VMEM_BYTES),
             name="step_kernel",
-        )(x_t.transpose(0, 2, 1), x_next.transpose(0, 2, 1), labels_t, learn_rate.reshape(1), mom_coef.reshape(1),
+        )(x_t.transpose(0, 2, 1), x_next.transpose(0, 2, 1), labels_t.reshape(1, 1), learn_rate.reshape(1, 1), mom_coef.reshape(1, 1),
           w_in, w_out.transpose(0, 2, 1), w_head, mom_in, mom_out.transpose(0, 2, 1), mom_head)
         stored = pl.pallas_call(
             store_kernel,

time: 73.9 us -> 73.4 us (level)
  no operation moved by 1% of the time
where the time goes in v4:
time: 73.4 us; the launch traced here: 73.3 us
  Pallas kernels  70.7 us (96%)
  between operations  2.58 us (4%)
    pallas_call x1, Pallas kernels, device_step(): pl.pallas_call(functools.partial(step_kernel, n_shards), out_shape=tuple(...  63.7 us
    pallas_call x1, Pallas kernels, device_step(): pl.pallas_call(store_kernel, out_shape=tuple((jax.ShapeDtypeStruct(shape,...  6.99 us

profile of v4, /device:TPU:0, one launch (start us, length us, event | category | flops | bytes accessed | tf_op | source)
XLA Modules:
  0.0 73.3 jit_solution(850441398131647893)
XLA Ops:
  2.6 63.7 %step_kernel.1 = (f32[8,192,768]{2,1,0:T(8,128)S(1)}, f32[8,192,768]{2,1,0:T(8,128)S(1)}, f32[192,1000]{1,0:T(8,128)S(1)}, f32[8,192,768]{2,1,0:T(8,128)S(1)}, f...) custom-call(bf16[1,192,576]{2,1,0:T(8,128)(2,1)} %bitcast.14, ...), custom_call_target="tpu_custom_call" | custom-call | tf_op jit(solution)/shard_map/step_kernel/pallas_call | solution.py:326
  66.3 7.0 %store_kernel.1 = (f32[8,192,768]{2,1,0:T(8,128)}, f32[8,192,768]{2,1,0:T(8,128)}, f32[192,1000]{1,0:T(8,128)}, f32[8,192,768]{2,1,0:T(8,128)}, f32[8,192,768]{2...) custom-call(f32[8,192,768]{2,1,0:T(8,128)S(1)} %get-tuple-element.21.refs_0_, ...), custom_call_target="tpu_custom_call" | custom-call | tf_op jit(solution)/shard_map/store_kernel/pallas_call | solution.py:360

commit v5 on v4

--- a/solution.py
+++ b/solution.py
@@ -47,11 +47,12 @@
 
 
 def step_kernel(n_shards,
-                x_ref, x_next_ref, label_ref, rate_ref, coef_ref, w_in_hbm, w_out_hbm, w_head_hbm, m_in_hbm, m_out_hbm, m_head_hbm,
+                x_hbm, x_next_hbm, label_hbm, rate_hbm, coef_hbm, w_in_hbm, w_out_hbm, w_head_hbm, m_in_hbm, m_out_hbm, m_head_hbm,
                 w_in_ref, w_out_ref, w_head_ref, m_in_ref, m_out_ref, m_head_ref, logits_ref,
                 stream, d_stream, x_hat, acts, pre_acts, hidden, d_branch, d_pre, w_in, w_out,
                 grads, recv0, recv1, recv2, sums, head_send, head_recv,
-                load_sem, mom_sem, send_sem, recv_sem, head_send_sem, head_recv_sem):
+                x_ref, x_next_ref, label_ref, rate_ref, coef_ref,
+                load_sem, mom_sem, small_sem, send_sem, recv_sem, head_send_sem, head_recv_sem):
     layers, tokens, mlp_dim = pre_acts.shape
     dim = stream.shape[1]
     classes = w_head_ref.shape[1]
@@ -76,24 +77,22 @@
                  pltpu.make_async_copy(m_in_hbm, m_in_ref, mom_sem.at[2]),
                  pltpu.make_async_copy(m_out_hbm, m_out_ref, mom_sem.at[3]))
 
-    for copy in load(0) + load(1):
+    small_loads = [pltpu.make_async_copy(src, dst, small_sem.at[i]) for i, (src, dst) in enumerate(
+        ((x_hbm, x_ref), (label_hbm, label_ref), (rate_hbm, rate_ref), (coef_hbm, coef_ref), (x_next_hbm, x_next_ref)))]
+
+    small_loads[0].start()
+    for layer in range(layers):
+        for copy in load(layer):
+            copy.start()
+    for copy in small_loads[1:] + [mom_loads[0]]:
         copy.start()
     for step in range(1, n_shards):
         other = (me + step) % n_shards
         pl.semaphore_signal(barrier, inc=1, device_id=(other // 2, other % 2), device_id_type=MESH)
+    small_loads[0].wait()
     stream[...] = x_ref[0].astype(F32).T
 
     def forward(layer, carry):
-        @pl.when(layer + 2 < layers)
-        def _():
-            for copy in load(layer + 2):
-                copy.start()
-
-        @pl.when(layer == layers - 2)
-        def _():
-            for copy in mom_loads:
-                copy.start()
-
         for copy in load(layer):
             copy.wait()
         w_in[layer] = w_in_ref[layer].astype(BF16)
@@ -110,9 +109,12 @@
         return carry
 
     lax.fori_loop(0, layers, forward, 0)
+    for copy in mom_loads[1:]:
+        copy.start()
 
     pooled = (jnp.sum(stream[...], axis=0, keepdims=True) * (1.0 / tokens)).astype(BF16)
-    mom_loads[0].wait()
+    for copy in small_loads[1:] + [mom_loads[0]]:
+        copy.wait()
     w_head = w_head_ref[...].astype(BF16)
     pooled_rows = jnp.broadcast_to(pooled.astype(F32), (16, dim)).astype(BF16)
     logits = dot(pooled_rows, w_head, NN)
@@ -326,7 +328,7 @@
         results = pl.pallas_call(
             functools.partial(step_kernel, n_shards),
             out_shape=tuple(pltpu.VMEM(shape, F32) for shape in shapes),
-            in_specs=[vmem] * 5 + [hbm] * 6,
+            in_specs=[hbm] * 11,
             out_specs=(vmem,) * 7,
             scratch_shapes=[
                 pltpu.VMEM((tokens, dim), F32),
@@ -346,8 +348,14 @@
                 pltpu.VMEM((layers, 2 * half, LANES), BF16),
                 pltpu.VMEM((16, LANES), F32),
                 pltpu.VMEM((n_shards, 16, LANES), F32),
+                pltpu.VMEM((1, dim, tokens), BF16),
+                pltpu.VMEM((1, dim, tokens), BF16),
+                pltpu.VMEM((1, 1), jnp.int32),
+                pltpu.VMEM((1, 1), F32),
+                pltpu.VMEM((1, 1), F32),
                 pltpu.SemaphoreType.DMA((layers, 2)),
                 pltpu.SemaphoreType.DMA((4,)),
+                pltpu.SemaphoreType.DMA((5,)),
                 pltpu.SemaphoreType.DMA((layers, 10)),
                 pltpu.SemaphoreType.DMA((layers, 10)),
                 pltpu.SemaphoreType.DMA((n_shards,)),

time: 73.4 us -> 74.8 us (1.019)
  Pallas kernels: 70.7 us -> 72.1 us
    pallas_call x1, Pallas kernels: 63.7 us -> 65.1 us  [device_step(): pl.pallas_call(functools.partial(step_kernel, n_shards), out_shape=tuple(...]
where the time goes in v5:
time: 74.8 us; the launch traced here: 74.7 us
  Pallas kernels  72.1 us (96%)
  between operations  2.58 us (3%)
    pallas_call x1, Pallas kernels, device_step(): pl.pallas_call(functools.partial(step_kernel, n_shards), out_shape=tuple(...  65.1 us
    pallas_call x1, Pallas kernels, device_step(): pl.pallas_call(store_kernel, out_shape=tuple((jax.ShapeDtypeStruct(shape,...  6.99 us

profile of v5, /device:TPU:0, one launch (start us, length us, event | category | flops | bytes accessed | tf_op | source)
XLA Modules:
  0.0 74.7 jit_solution(5002854948001046090)
XLA Ops:
  2.6 65.1 %step_kernel.1 = (f32[8,192,768]{2,1,0:T(8,128)S(1)}, f32[8,192,768]{2,1,0:T(8,128)S(1)}, f32[192,1000]{1,0:T(8,128)S(1)}, f32[8,192,768]{2,1,0:T(8,128)S(1)}, f...) custom-call(bf16[1,192,576]{2,1,0:T(8,128)(2,1)} %bitcast.14, ...), custom_call_target="tpu_custom_call" | custom-call | tf_op jit(solution)/shard_map/step_kernel/pallas_call | solution.py:328
  67.7 7.0 %store_kernel.1 = (f32[8,192,768]{2,1,0:T(8,128)}, f32[8,192,768]{2,1,0:T(8,128)}, f32[192,1000]{1,0:T(8,128)}, f32[8,192,768]{2,1,0:T(8,128)}, f32[8,192,768]{2...) custom-call(f32[8,192,768]{2,1,0:T(8,128)S(1)} %get-tuple-element.21.refs_0_, ...), custom_call_target="tpu_custom_call" | custom-call | tf_op jit(solution)/shard_map/store_kernel/pallas_call | solution.py:368

commit v6 on v5

--- a/solution.py
+++ b/solution.py
@@ -81,10 +81,7 @@
         ((x_hbm, x_ref), (label_hbm, label_ref), (rate_hbm, rate_ref), (coef_hbm, coef_ref), (x_next_hbm, x_next_ref)))]
 
     small_loads[0].start()
-    for layer in range(layers):
-        for copy in load(layer):
-            copy.start()
-    for copy in small_loads[1:] + [mom_loads[0]]:
+    for copy in load(0) + load(1):
         copy.start()
     for step in range(1, n_shards):
         other = (me + step) % n_shards
@@ -95,6 +92,17 @@
     def forward(layer, carry):
         for copy in load(layer):
             copy.wait()
+
+        @pl.when(layer + 2 < layers)
+        def _():
+            for copy in load(layer + 2):
+                copy.start()
+
+        @pl.when(layer == layers - 2)
+        def _():
+            for copy in small_loads[1:] + [mom_loads[0]]:
+                copy.start()
+
         w_in[layer] = w_in_ref[layer].astype(BF16)
         w_out[layer] = w_out_ref[layer].astype(BF16)
         for part in parts:

time: 74.8 us -> 72.8 us (0.973)
  Pallas kernels: 72.1 us -> 70.1 us
    pallas_call x1, Pallas kernels: 65.1 us -> 63.1 us  [device_step(): pl.pallas_call(functools.partial(step_kernel, n_shards), out_shape=tuple(...]
where the time goes in v6:
time: 72.8 us; the launch traced here: 72.7 us
  Pallas kernels  70.1 us (96%)
  between operations  2.58 us (4%)
    pallas_call x1, Pallas kernels, device_step(): pl.pallas_call(functools.partial(step_kernel, n_shards), out_shape=tuple(...  63.1 us
    pallas_call x1, Pallas kernels, device_step(): pl.pallas_call(store_kernel, out_shape=tuple((jax.ShapeDtypeStruct(shape,...  6.99 us

profile of v6, /device:TPU:0, one launch (start us, length us, event | category | flops | bytes accessed | tf_op | source)
XLA Modules:
  0.0 72.7 jit_solution(9014261398233168090)
XLA Ops:
  2.6 63.1 %step_kernel.1 = (f32[8,192,768]{2,1,0:T(8,128)S(1)}, f32[8,192,768]{2,1,0:T(8,128)S(1)}, f32[192,1000]{1,0:T(8,128)S(1)}, f32[8,192,768]{2,1,0:T(8,128)S(1)}, f...) custom-call(bf16[1,192,576]{2,1,0:T(8,128)(2,1)} %bitcast.14, ...), custom_call_target="tpu_custom_call" | custom-call | tf_op jit(solution)/shard_map/step_kernel/pallas_call | solution.py:336
  65.7 7.0 %store_kernel.1 = (f32[8,192,768]{2,1,0:T(8,128)}, f32[8,192,768]{2,1,0:T(8,128)}, f32[192,1000]{1,0:T(8,128)}, f32[8,192,768]{2,1,0:T(8,128)}, f32[8,192,768]{2...) custom-call(f32[8,192,768]{2,1,0:T(8,128)S(1)} %get-tuple-element.21.refs_0_, ...), custom_call_target="tpu_custom_call" | custom-call | tf_op jit(solution)/shard_map/store_kernel/pallas_call | solution.py:376

commit v7 on v6

--- a/solution.py
+++ b/solution.py
@@ -18,8 +18,9 @@
 NT = (((1,), (1,)), ((), ()))
 NN = (((1,), (0,)), ((), ()))
 TN = (((0,), (0,)), ((), ()))
-VMEM_BYTES = 46 * 1000 * 1000
+VMEM_BYTES = 40600 * 1000
 ROWS = 192
+LATE = 3
 
 
 def dot(a, b, dims):
@@ -39,18 +40,43 @@
     return inner, 0.5 + 0.5 * jnp.tanh(pre * inner)
 
 
-AFTER_BACKWARD = [[], [(0, 0)], [(0, 1)], [(0, 2)], [(1, 0), (0, 3)], [(1, 1), (0, 4)], [(0, 5)], []]
-BEFORE_HEAD = [(0, 6), (0, 7), (2, 1), (1, 5), (1, 4), (1, 6), (2, 0), (1, 7), (1, 3), (1, 2), (2, 5), (2, 6), (2, 7), (2, 4), (2, 3), (2, 2), (3, 5), (3, 7), (3, 6)]
-AFTER_HEAD = [(4, 5), (3, 4), (5, 5), (3, 3), (3, 2), (4, 7), (4, 6), (5, 7)]
-BEFORE_UPDATE = [[], [(5, 6)], [], [(5, 4), (4, 3)], [(4, 2), (5, 3)], [(5, 2), (4, 1)], [(4, 0), (5, 1)], [(5, 0)]]
-AFTER_UPDATE = [[(3, 1), (3, 0)], [(4, 4)], [], [], [], [], [], []]
+AFTER_BACKWARD = [[], [(0, 0)], [(0, 1)], [(0, 2), (1, 0)], [(1, 1), (0, 3)], [(1, 2), (0, 4)], [(0, 5), (2, 1), (1, 3), (0, 6)], []]
+BEFORE_HEAD = [(1, 5), (0, 7), (2, 3), (1, 6), (2, 5), (1, 4), (1, 7), (2, 2), (2, 6), (2, 0), (2, 4), (2, 7), (3, 5), (3, 6), (3, 7)]
+AFTER_HEAD = [(3, 4), (3, 3), (4, 7), (3, 1), (4, 5), (4, 4), (3, 2), (5, 7), (4, 6)]
+BEFORE_UPDATE = [[], [(5, 4), (5, 5), (3, 0), (5, 6)], [(4, 3), (4, 1)], [(5, 3), (4, 2)], [(4, 0)]]
+AFTER_UPDATE = [[], [], [], [], [(5, 2)]]
+AT_END = [(5, 1), (5, 0)]
+
+
+def update(layer, slot, rate, coef, sums, old, new, w_in, w_out):
+    dim, mlp_dim = w_in.shape
+    half = mlp_dim // LANES * dim
+    for start in range(0, mlp_dim, LANES):
+        lanes = slice(start, start + LANES)
+        for base, w_old, m_old, w_new, m_new, w_bf in (
+                (0, old[0], old[1], new[0], new[1], w_in), (half, old[2], old[3], new[2], new[3], w_out)):
+            row = base + start // LANES * dim
+            moment = coef * m_old[layer, :, lanes] + sums[layer, row:row + dim].astype(F32)
+            m_new[slot, :, lanes] = moment
+            weight = w_old[layer, :, lanes] - rate * moment
+            w_new[slot, :, lanes] = weight
+            w_bf[:, lanes] = weight.astype(BF16)
+
+
+def next_block(stream, w_in, w_out):
+    for start in range(0, stream.shape[0], ROWS):
+        part = slice(start, start + ROWS)
+        stream_in = stream[part]
+        pre = dot(normalize(stream_in)[0].astype(BF16), w_in[...], NN)
+        out = (pre * gelu_parts(pre)[1]).astype(BF16)
+        stream[part] = stream_in + dot(out, w_out[...], NT)
 
 
 def step_kernel(n_shards,
                 x_hbm, x_next_hbm, label_hbm, rate_hbm, coef_hbm, w_in_hbm, w_out_hbm, w_head_hbm, m_in_hbm, m_out_hbm, m_head_hbm,
-                w_in_ref, w_out_ref, w_head_ref, m_in_ref, m_out_ref, m_head_ref, logits_ref,
-                stream, d_stream, x_hat, acts, pre_acts, hidden, d_branch, d_pre, w_in, w_out,
-                grads, recv0, recv1, recv2, sums, head_send, head_recv,
+                w_in_ref, w_out_ref, w_head_ref, m_in_ref, m_out_ref, m_head_ref, sums, stream,
+                d_stream, x_hat, acts, pre_acts, hidden, d_branch, d_pre, w_in, w_out,
+                grads, recv0, recv1, recv2, head_send, head_recv,
                 x_ref, x_next_ref, label_ref, rate_ref, coef_ref,
                 load_sem, mom_sem, small_sem, send_sem, recv_sem, head_send_sem, head_recv_sem):
     layers, tokens, mlp_dim = pre_acts.shape
@@ -69,8 +95,8 @@
     me = inner * 2 + core
 
     def load(layer):
-        return (pltpu.make_async_copy(w_in_hbm.at[layer], w_in_ref.at[layer], load_sem.at[layer, 0]),
-                pltpu.make_async_copy(w_out_hbm.at[layer], w_out_ref.at[layer], load_sem.at[layer, 1]))
+        return (pltpu.make_async_copy(w_in_hbm.at[layer], w_in_ref.at[layer], load_sem.at[layer % 4, 0]),
+                pltpu.make_async_copy(w_out_hbm.at[layer], w_out_ref.at[layer], load_sem.at[layer % 4, 1]))
 
     mom_loads = (pltpu.make_async_copy(w_head_hbm, w_head_ref, mom_sem.at[0]),
                  pltpu.make_async_copy(m_head_hbm, m_head_ref, mom_sem.at[1]),
@@ -149,18 +175,25 @@
     def head_copy(step):
         other = (me + step) % n_shards
         return pltpu.make_async_remote_copy(
-            src_ref=head_send, dst_ref=head_recv.at[step], send_sem=head_send_sem.at[step],
-            recv_sem=head_recv_sem.at[step], device_id=(other // 2, other % 2), device_id_type=MESH)
+            src_ref=head_send, dst_ref=head_recv.at[step], send_sem=head_send_sem.at[0],
+            recv_sem=head_recv_sem.at[0], device_id=(other // 2, other % 2), device_id_type=MESH)
 
     for step in range(1, n_shards):
         head_copy(step).start()
 
+    def all_head_copies():
+        others = head_recv.at[pl.ds(1, n_shards - 1)]
+        return pltpu.make_async_remote_copy(
+            src_ref=others, dst_ref=others, send_sem=head_send_sem.at[0],
+            recv_sem=head_recv_sem.at[0], device_id=peer_core, device_id_type=MESH)
+
     mine = half * core
     place_a, place_b = mine, mine + half // 2
 
-    def remote(src, dst, layer, sem, device):
+    def remote(src, dst, layer, stage, device):
+        near = 0 if stage in (0, 5) else 1
         return pltpu.make_async_remote_copy(
-            src_ref=src, dst_ref=dst, send_sem=send_sem.at[layer, sem], recv_sem=recv_sem.at[layer, sem],
+            src_ref=src, dst_ref=dst, send_sem=send_sem.at[layer, near], recv_sem=recv_sem.at[layer, stage],
             device_id=device, device_id_type=MESH)
 
     def copies(stage, layer):
@@ -171,23 +204,23 @@
             return sums.at[layer, pl.ds(start, size)]
 
         if stage == 0:
-            return [remote(grad(half * (1 - core), half), recv0.at[layer], layer, 0, peer_core)]
+            return [remote(grad(half * (1 - core), half), recv0.at[layer], layer, stage, peer_core)]
         if stage == 1:
-            return [remote(grad(place_a + quarter * (1 - x), quarter), recv1.at[layer, 0], layer, 1, peer_x),
-                    remote(grad(place_b + quarter * (1 - y), quarter), recv1.at[layer, 1], layer, 2, peer_y)]
+            return [remote(grad(place_a + quarter * (1 - x), quarter), recv1.at[layer, 0], layer, stage, peer_x),
+                    remote(grad(place_b + quarter * (1 - y), quarter), recv1.at[layer, 1], layer, stage, peer_y)]
         if stage == 2:
-            return [remote(grad(place_a + quarter * x + eighth * (1 - y), eighth), recv2.at[layer, 0], layer, 3, peer_y),
-                    remote(grad(place_b + quarter * y + eighth * (1 - x), eighth), recv2.at[layer, 1], layer, 4, peer_x)]
+            return [remote(grad(place_a + quarter * x + eighth * (1 - y), eighth), recv2.at[layer, 0], layer, stage, peer_y),
+                    remote(grad(place_b + quarter * y + eighth * (1 - x), eighth), recv2.at[layer, 1], layer, stage, peer_x)]
         if stage == 3:
             spot_a = total(place_a + quarter * x + eighth * y, eighth)
             spot_b = total(place_b + quarter * y + eighth * x, eighth)
-            return [remote(spot_a, spot_a, layer, 5, peer_y), remote(spot_b, spot_b, layer, 6, peer_x)]
+            return [remote(spot_a, spot_a, layer, stage, peer_y), remote(spot_b, spot_b, layer, stage, peer_x)]
         if stage == 4:
             spot_a = total(place_a + quarter * x, quarter)
             spot_b = total(place_b + quarter * y, quarter)
-            return [remote(spot_a, spot_a, layer, 7, peer_x), remote(spot_b, spot_b, layer, 8, peer_y)]
+            return [remote(spot_a, spot_a, layer, stage, peer_x), remote(spot_b, spot_b, layer, stage, peer_y)]
         spot = total(mine, half)
-        return [remote(spot, spot, layer, 9, peer_core)]
+        return [remote(spot, spot, layer, stage, peer_core)]
 
     def add(layer, dst, start, size, other):
         dst[layer, pl.ds(start, size)] = (
@@ -199,8 +232,9 @@
 
     def advance(stage, turn):
         layer = layers - 1 - turn
-        for copy in copies(stage, layer):
-            copy.wait_recv()
+        size = (half, 2 * quarter, 2 * eighth, 2 * eighth, 2 * quarter, half)[stage]
+        spot = grads.at[layer, pl.ds(0, size)]
+        remote(spot, spot, layer, stage, peer_core).wait_recv()
         if stage == 0:
             add(layer, grads, mine, half, recv0.at[layer])
         elif stage == 1:
@@ -253,8 +287,7 @@
     run(BEFORE_HEAD)
 
     rate, coef = rate_ref[...], coef_ref[...]
-    for step in range(1, n_shards):
-        head_copy(step).wait_recv()
+    all_head_copies().wait_recv()
     for copy in mom_loads[1:]:
         copy.wait()
     columns = []
@@ -278,44 +311,62 @@
 
     def next_forward(layer, carry):
         run_at(layer, BEFORE_UPDATE)
-        for chunk in range(chunks):
-            lanes = slice(chunk * LANES, (chunk + 1) * LANES)
-            for base, w_ref, m_ref, w_bf in ((0, w_in_ref, m_in_ref, w_in), (half, w_out_ref, m_out_ref, w_out)):
-                grad = sums[layer, base + chunk * dim:base + (chunk + 1) * dim].astype(F32)
-                moment = coef * m_ref[layer, :, lanes] + grad
-                m_ref[layer, :, lanes] = moment
-                weight = w_ref[layer, :, lanes] - rate * moment
-                w_ref[layer, :, lanes] = weight
-                w_bf[layer, :, lanes] = weight.astype(BF16)
+        update(layer, layer, rate, coef, sums, (w_in_ref, m_in_ref, w_out_ref, m_out_ref), (w_in_ref, m_in_ref, w_out_ref, m_out_ref),
+               w_in.at[layer], w_out.at[layer])
         run_at(layer, AFTER_UPDATE)
-        for part in parts:
-            stream_in = stream[part]
-            pre = dot(normalize(stream_in)[0].astype(BF16), w_in[layer], NN)
-            out = (pre * gelu_parts(pre)[1]).astype(BF16)
-            stream[part] = stream_in + dot(out, w_out[layer], NT)
+        next_block(stream, w_in.at[layer], w_out.at[layer])
         return carry
 
-    lax.fori_loop(0, layers, next_forward, 0)
+    lax.fori_loop(0, layers - LATE, next_forward, 0)
+    run(AT_END)
+
+    def finish_all(layer, carry):
+        for stage, size in ((0, 2 * half), (1, 3 * half // 2)):
+            spot = grads.at[layer, pl.ds(0, size)]
+            remote(spot, spot, layer, stage, peer_core).wait_send()
+        return carry
+
+    lax.fori_loop(0, layers, finish_all, 0)
+    all_head_copies().wait_send()
+
+
+def store_kernel(rate_ref, coef_ref, w_in_ref, w_out_ref, w_head_ref, m_in_ref, m_out_ref, m_head_ref, sums, stream_ref,
+                 w_in_out, w_out_out, w_head_out, m_in_out, m_out_out, m_head_out, logits_out,
+                 stream, w_in_late, m_in_late, w_out_late, m_out_late, w_in, w_out, logits, early_sem, late_sem):
+    layers = w_in_ref.shape[0]
+    tokens, dim = stream.shape
+    early = layers - LATE
+    rate, coef = rate_ref[...], coef_ref[...]
+    old = (w_in_ref, m_in_ref, w_out_ref, m_out_ref)
+    new = (w_in_late, m_in_late, w_out_late, m_out_late)
+    outs = (w_in_out, m_in_out, w_out_out, m_out_out)
+    copies = [pltpu.make_async_copy(src.at[pl.ds(0, early)], dst.at[pl.ds(0, early)], early_sem.at[i])
+              for i, (src, dst) in enumerate(zip(old, outs))]
+    copies.append(pltpu.make_async_copy(w_head_ref, w_head_out, early_sem.at[4]))
+    copies.append(pltpu.make_async_copy(m_head_ref, m_head_out, early_sem.at[5]))
+    for copy in copies:
+        copy.start()
+    stream[...] = stream_ref[...]
+
+    def late_copies(step):
+        return [pltpu.make_async_copy(src.at[step], dst.at[early + step], late_sem.at[step, i])
+                for i, (src, dst) in enumerate(zip(new, outs))]
+
+    def late_layer(step, carry):
+        update(early + step, step, rate, coef, sums, old, new, w_in, w_out)
+        for copy in late_copies(step):
+            copy.start()
+        next_block(stream, w_in, w_out)
+        return carry
+
+    lax.fori_loop(0, LATE, late_layer, 0)
     pooled = jnp.sum(stream[...], axis=0, keepdims=True) * (1.0 / tokens)
     pooled = jnp.broadcast_to(pooled, (16, dim)).astype(BF16)
-    logits_ref[...] = dot(pooled, w_head_ref[...].astype(BF16), NN)[0:1]
-
-    def finish_all(layer, carry):
-        for stage in range(6):
-            for copy in copies(stage, layer):
-                copy.wait_send()
-        return carry
-
-    lax.fori_loop(0, layers, finish_all, 0)
-    for step in range(1, n_shards):
-        head_copy(step).wait_send()
-
-
-def store_kernel(*refs):
-    count = (len(refs) - 1) // 2
-    copies = [pltpu.make_async_copy(refs[i], refs[count + i], refs[-1].at[i]) for i in range(count)]
-    for copy in copies:
-        copy.start()
+    logits[...] = dot(pooled, w_head_ref[...].astype(BF16), NN)[0:1]
+    copies.append(pltpu.make_async_copy(logits, logits_out, early_sem.at[6]))
+    copies[-1].start()
+    for step in range(LATE):
+        copies += late_copies(step)
     for copy in copies:
         copy.wait()
 
@@ -332,14 +383,14 @@
         half = mlp_dim // LANES * dim
         vmem = pl.BlockSpec(memory_space=pltpu.VMEM)
         hbm = pl.BlockSpec(memory_space=pl.ANY)
-        shapes = [(layers, dim, mlp_dim), (layers, dim, mlp_dim), (dim, classes)] * 2 + [(1, classes)]
+        shapes = [(layers, dim, mlp_dim), (layers, dim, mlp_dim), (dim, classes)] * 2
+        rate, coef = learn_rate.reshape(1, 1), mom_coef.reshape(1, 1)
         results = pl.pallas_call(
             functools.partial(step_kernel, n_shards),
-            out_shape=tuple(pltpu.VMEM(shape, F32) for shape in shapes),
+            out_shape=tuple(pltpu.VMEM(shape, F32) for shape in shapes) + (pltpu.VMEM((layers, 2 * half, LANES), BF16), pltpu.VMEM((tokens, dim), F32)),
             in_specs=[hbm] * 11,
-            out_specs=(vmem,) * 7,
+            out_specs=(vmem,) * 8,
             scratch_shapes=[
-                pltpu.VMEM((tokens, dim), F32),
                 pltpu.VMEM((tokens, dim), F32),
                 pltpu.VMEM((layers, tokens, dim + 1), F32),
                 pltpu.VMEM((tokens, dim), BF16),
@@ -353,7 +404,6 @@
                 pltpu.VMEM((layers, half, LANES), BF16),
                 pltpu.VMEM((layers, 2, half // 4, LANES), BF16),
                 pltpu.VMEM((layers, 2, half // 8, LANES), BF16),
-                pltpu.VMEM((layers, 2 * half, LANES), BF16),
                 pltpu.VMEM((16, LANES), F32),
                 pltpu.VMEM((n_shards, 16, LANES), F32),
                 pltpu.VMEM((1, dim, tokens), BF16),
@@ -361,28 +411,32 @@
                 pltpu.VMEM((1, 1), jnp.int32),
                 pltpu.VMEM((1, 1), F32),
                 pltpu.VMEM((1, 1), F32),
-                pltpu.SemaphoreType.DMA((layers, 2)),
+                pltpu.SemaphoreType.DMA((4, 2)),
                 pltpu.SemaphoreType.DMA((4,)),
                 pltpu.SemaphoreType.DMA((5,)),
-                pltpu.SemaphoreType.DMA((layers, 10)),
-                pltpu.SemaphoreType.DMA((layers, 10)),
-                pltpu.SemaphoreType.DMA((n_shards,)),
-                pltpu.SemaphoreType.DMA((n_shards,)),
+                pltpu.SemaphoreType.DMA((layers, 2)),
+                pltpu.SemaphoreType.DMA((layers, 6)),
+                pltpu.SemaphoreType.DMA((1,)),
+                pltpu.SemaphoreType.DMA((1,)),
             ],
             compiler_params=pltpu.CompilerParams(collective_id=0, has_side_effects=True, vmem_limit_bytes=VMEM_BYTES),
             name="step_kernel",
-        )(x_t.transpose(0, 2, 1), x_next.transpose(0, 2, 1), labels_t.reshape(1, 1), learn_rate.reshape(1, 1), mom_coef.reshape(1, 1),
+        )(x_t.transpose(0, 2, 1), x_next.transpose(0, 2, 1), labels_t.reshape(1, 1), rate, coef,
           w_in, w_out.transpose(0, 2, 1), w_head, mom_in, mom_out.transpose(0, 2, 1), mom_head)
-        stored = pl.pallas_call(
+        late = pltpu.VMEM((LATE, dim, mlp_dim), F32)
+        w_in_new, w_out_new, w_head_new, m_in_new, m_out_new, m_head_new, logits = pl.pallas_call(
             store_kernel,
-            out_shape=tuple(jax.ShapeDtypeStruct(shape, F32) for shape in shapes),
-            in_specs=[vmem] * 7,
+            out_shape=tuple(jax.ShapeDtypeStruct(shape, F32) for shape in shapes + [(1, classes)]),
+            in_specs=[vmem] * 10,
             out_specs=(hbm,) * 7,
-            scratch_shapes=[pltpu.SemaphoreType.DMA((7,))],
-            compiler_params=pltpu.CompilerParams(vmem_limit_bytes=1000 * 1000),
+            scratch_shapes=[
+                pltpu.VMEM((tokens, dim), F32), late, late, late, late,
+                pltpu.VMEM((dim, mlp_dim), BF16), pltpu.VMEM((dim, mlp_dim), BF16), pltpu.VMEM((1, classes), F32),
+                pltpu.SemaphoreType.DMA((7,)), pltpu.SemaphoreType.DMA((LATE, 4)),
+            ],
+            compiler_params=pltpu.CompilerParams(vmem_limit_bytes=11 * 1000 * 1000),
             name="store_kernel",
-        )(*results)
-        w_in_new, w_out_new, w_head_new, m_in_new, m_out_new, m_head_new, logits = stored
+        )(rate, coef, *results)
         return (logits, w_in_new, w_out_new.transpose(0, 2, 1), w_head_new,
                 m_in_new, m_out_new.transpose(0, 2, 1), m_head_new)
 

time: 72.8 us -> 69.4 us (0.953)
  Pallas kernels: 70.1 us -> 66.7 us
    pallas_call x1, Pallas kernels: 63.1 us -> 59.5 us  [device_step(): pl.pallas_call(functools.partial(step_kernel, n_shards), out_shape=tuple(...]
where the time goes in v7:
time: 69.4 us; the launch traced here: 69.3 us
  Pallas kernels  66.7 us (96%)
  between operations  2.58 us (4%)
    pallas_call x1, Pallas kernels, device_step(): pl.pallas_call(functools.partial(step_kernel, n_shards), out_shape=tuple(...  59.5 us
    pallas_call x1, Pallas kernels, device_step(): pl.pallas_call(store_kernel, out_shape=tuple((jax.ShapeDtypeStruct(shape,...  7.13 us

profile of v7, /device:TPU:0, one launch (start us, length us, event | category | flops | bytes accessed | tf_op | source)
XLA Modules:
  0.0 69.3 jit_solution(11983401458127114101)
XLA Ops:
  2.6 59.5 %step_kernel.1 = (f32[8,192,768]{2,1,0:T(8,128)S(1)}, f32[8,192,768]{2,1,0:T(8,128)S(1)}, f32[192,1000]{1,0:T(8,128)S(1)}, f32[8,192,768]{2,1,0:T(8,128)S(1)}, f...) custom-call(bf16[1,192,576]{2,1,0:T(8,128)(2,1)} %bitcast.16, ...), custom_call_target="tpu_custom_call" | custom-call | tf_op jit(solution)/shard_map/step_kernel/pallas_call | solution.py:388
  62.1 7.1 %store_kernel.1 = (f32[8,192,768]{2,1,0:T(8,128)}, f32[8,192,768]{2,1,0:T(8,128)}, f32[192,1000]{1,0:T(8,128)}, f32[8,192,768]{2,1,0:T(8,128)}, f32[8,192,768]{2...) custom-call(f32[1,1]{1,0:T(1,128)} %bitcast.11.rate_ref, f32[1,1]{1,0:T(1,128)} %bitcast.13.coef_ref, ...), custom_call_target="tpu_custom_call" | custom-call | tf_op jit(solution)/shard_map/store_kernel/pallas_call | solution.py:427

commit v8 on v7

--- a/solution.py
+++ b/solution.py
@@ -35,9 +35,10 @@
     return centered * rstd, rstd
 
 
-def gelu_parts(pre):
-    inner = GELU_SCALE + (GELU_SCALE * GELU_CUBIC) * (pre * pre)
-    return inner, 0.5 + 0.5 * jnp.tanh(pre * inner)
+def gelu_parts(pre_half):
+    square = pre_half * pre_half
+    tanh_val = jnp.tanh(pre_half * (2.0 * GELU_SCALE + (8.0 * GELU_SCALE * GELU_CUBIC) * square))
+    return square, tanh_val, 1.0 + tanh_val
 
 
 AFTER_BACKWARD = [[], [(0, 0)], [(0, 1)], [(0, 2), (1, 0)], [(1, 1), (0, 3)], [(1, 2), (0, 4)], [(0, 5), (2, 1), (1, 3), (0, 6)], []]
@@ -53,22 +54,22 @@
     half = mlp_dim // LANES * dim
     for start in range(0, mlp_dim, LANES):
         lanes = slice(start, start + LANES)
-        for base, w_old, m_old, w_new, m_new, w_bf in (
-                (0, old[0], old[1], new[0], new[1], w_in), (half, old[2], old[3], new[2], new[3], w_out)):
+        for base, w_old, m_old, w_new, m_new, w_bf, scale in (
+                (0, old[0], old[1], new[0], new[1], w_in, 0.5), (half, old[2], old[3], new[2], new[3], w_out, 1.0)):
             row = base + start // LANES * dim
             moment = coef * m_old[layer, :, lanes] + sums[layer, row:row + dim].astype(F32)
             m_new[slot, :, lanes] = moment
             weight = w_old[layer, :, lanes] - rate * moment
             w_new[slot, :, lanes] = weight
-            w_bf[:, lanes] = weight.astype(BF16)
+            w_bf[:, lanes] = (weight * scale).astype(BF16)
 
 
 def next_block(stream, w_in, w_out):
     for start in range(0, stream.shape[0], ROWS):
         part = slice(start, start + ROWS)
         stream_in = stream[part]
-        pre = dot(normalize(stream_in)[0].astype(BF16), w_in[...], NN)
-        out = (pre * gelu_parts(pre)[1]).astype(BF16)
+        pre_half = dot(normalize(stream_in)[0].astype(BF16), w_in[...], NN)
+        out = (pre_half * gelu_parts(pre_half)[2]).astype(BF16)
         stream[part] = stream_in + dot(out, w_out[...], NT)
 
 
@@ -115,34 +116,37 @@
     small_loads[0].wait()
     stream[...] = x_ref[0].astype(F32).T
 
-    def forward(layer, carry):
-        for copy in load(layer):
+    def forward(pair, carry):
+        first = 2 * pair
+        for copy in load(first) + load(first + 1):
             copy.wait()
 
-        @pl.when(layer + 2 < layers)
+        @pl.when(first + 2 < layers)
         def _():
-            for copy in load(layer + 2):
+            for copy in load(first + 2) + load(first + 3):
                 copy.start()
 
-        @pl.when(layer == layers - 2)
+        @pl.when(first + 2 >= layers)
         def _():
             for copy in small_loads[1:] + [mom_loads[0]]:
                 copy.start()
 
-        w_in[layer] = w_in_ref[layer].astype(BF16)
-        w_out[layer] = w_out_ref[layer].astype(BF16)
-        for part in parts:
-            stream_in = stream[part]
-            normed, rstd = normalize(stream_in)
-            x_hat[layer, part, 0:dim] = normed
-            x_hat[layer, part, dim:dim + 1] = rstd
-            pre = dot(normed.astype(BF16), w_in[layer], NN)
-            pre_acts[layer, part] = pre
-            out = (pre * gelu_parts(pre)[1]).astype(BF16)
-            stream[part] = stream_in + dot(out, w_out[layer], NT)
+        for layer in (first, first + 1):
+            w_in[layer] = (0.5 * w_in_ref[layer]).astype(BF16)
+            w_out[layer] = w_out_ref[layer].astype(BF16)
+        for layer in (first, first + 1):
+            for part in parts:
+                stream_in = stream[part]
+                normed, rstd = normalize(stream_in)
+                x_hat[layer, part, 0:dim] = normed
+                x_hat[layer, part, dim:dim + 1] = rstd
+                pre_half = dot(normed.astype(BF16), w_in[layer], NN)
+                pre_acts[layer, part] = pre_half
+                out = (pre_half * gelu_parts(pre_half)[2]).astype(BF16)
+                stream[part] = stream_in + dot(out, w_out[layer], NT)
         return carry
 
-    lax.fori_loop(0, layers, forward, 0)
+    lax.fori_loop(0, layers // 2, forward, 0)
     for copy in mom_loads[1:]:
         copy.start()
 
@@ -262,10 +266,11 @@
             d_branch[part] = branch
             normed = x_hat[layer, part, 0:dim]
             acts[part] = normed.astype(BF16)
-            pre = pre_acts[layer, part]
-            inner_val, cdf = gelu_parts(pre)
-            hidden[part] = (pre * cdf).astype(BF16)
-            slope = cdf + ((cdf - cdf * cdf) * pre) * (6.0 * inner_val - 4.0 * GELU_SCALE)
+            pre_half = pre_acts[layer, part]
+            square, tanh_val, twice_cdf = gelu_parts(pre_half)
+            hidden[part] = (pre_half * twice_cdf).astype(BF16)
+            slope = twice_cdf + ((1.0 - tanh_val * tanh_val) * pre_half) * (
+                2.0 * GELU_SCALE + (24.0 * GELU_SCALE * GELU_CUBIC) * square)
             d_hidden = dot(branch, w_out[layer], NN).astype(BF16).astype(F32)
             d_pre_part = (d_hidden * slope).astype(BF16)
             d_pre[part] = d_pre_part
@@ -273,7 +278,7 @@
             mean_d = jnp.mean(d_act, axis=-1, keepdims=True)
             mean_dx = jnp.mean(d_act * normed, axis=-1, keepdims=True)
             d_stream[part] = d_stream[part] + x_hat[layer, part, dim:dim + 1] * (d_act - mean_d - normed * mean_dx)
-        g_in = dot(acts[...], d_pre[...], TN).astype(BF16)
+        g_in = (0.5 * dot(acts[...], d_pre[...], TN)).astype(BF16)
         g_out = dot(d_branch[...], hidden[...], TN).astype(BF16)
         for chunk in range(chunks):
             grads[layer, chunk * dim:(chunk + 1) * dim] = g_in[:, chunk * LANES:(chunk + 1) * LANES]

time: 69.4 us -> 68.1 us (0.981)
  Pallas kernels: 66.7 us -> 65.3 us
    pallas_call x1, Pallas kernels: 59.5 us -> 58.2 us  [device_step(): pl.pallas_call(functools.partial(step_kernel, n_shards), out_shape=tuple(...]
where the time goes in v8:
time: 68.1 us; the launch traced here: 67.9 us
  Pallas kernels  65.3 us (96%)
  between operations  2.58 us (4%)
    pallas_call x1, Pallas kernels, device_step(): pl.pallas_call(functools.partial(step_kernel, n_shards), out_shape=tuple(...  58.2 us
    pallas_call x1, Pallas kernels, device_step(): pl.pallas_call(store_kernel, out_shape=tuple((jax.ShapeDtypeStruct(shape,...  7.13 us

profile of v8, /device:TPU:0, one launch (start us, length us, event | category | flops | bytes accessed | tf_op | source)
XLA Modules:
  0.0 67.9 jit_solution(2590413200978826977)
XLA Ops:
  2.6 58.2 %step_kernel.1 = (f32[8,192,768]{2,1,0:T(8,128)S(1)}, f32[8,192,768]{2,1,0:T(8,128)S(1)}, f32[192,1000]{1,0:T(8,128)S(1)}, f32[8,192,768]{2,1,0:T(8,128)S(1)}, f...) custom-call(bf16[1,192,576]{2,1,0:T(8,128)(2,1)} %bitcast.16, ...), custom_call_target="tpu_custom_call" | custom-call | tf_op jit(solution)/shard_map/step_kernel/pallas_call | solution.py:393
  60.8 7.1 %store_kernel.1 = (f32[8,192,768]{2,1,0:T(8,128)}, f32[8,192,768]{2,1,0:T(8,128)}, f32[192,1000]{1,0:T(8,128)}, f32[8,192,768]{2,1,0:T(8,128)}, f32[8,192,768]{2...) custom-call(f32[1,1]{1,0:T(1,128)} %bitcast.11.rate_ref, f32[1,1]{1,0:T(1,128)} %bitcast.13.coef_ref, ...), custom_call_target="tpu_custom_call" | custom-call | tf_op jit(solution)/shard_map/store_kernel/pallas_call | solution.py:432

commit v9 on v8

--- a/solution.py
+++ b/solution.py
@@ -174,16 +174,12 @@
     head_send[9:10, 0:dim - LANES] = pooled[:, LANES:dim]
     head_recv[0] = head_send[...]
 
-    pl.semaphore_wait(barrier, n_shards - 1)
 
     def head_copy(step):
         other = (me + step) % n_shards
         return pltpu.make_async_remote_copy(
             src_ref=head_send, dst_ref=head_recv.at[step], send_sem=head_send_sem.at[0],
             recv_sem=head_recv_sem.at[0], device_id=(other // 2, other % 2), device_id_type=MESH)
-
-    for step in range(1, n_shards):
-        head_copy(step).start()
 
     def all_head_copies():
         others = head_recv.at[pl.ds(1, n_shards - 1)]
@@ -259,8 +255,7 @@
             if steps:
                 pl.when(index == at)(functools.partial(run, steps))
 
-    def backward(turn, carry):
-        layer = layers - 1 - turn
+    def block_gradients(layer):
         for part in (slice(0, tokens),):
             branch = d_stream[part].astype(BF16)
             d_branch[part] = branch
@@ -283,11 +278,19 @@
         for chunk in range(chunks):
             grads[layer, chunk * dim:(chunk + 1) * dim] = g_in[:, chunk * LANES:(chunk + 1) * LANES]
             grads[layer, half + chunk * dim:half + (chunk + 1) * dim] = g_out[:, chunk * LANES:(chunk + 1) * LANES]
+
+    def backward(turn, carry):
+        block_gradients(layers - 1 - turn)
         start(0, turn)
         run_at(turn, AFTER_BACKWARD)
         return carry
 
-    lax.fori_loop(0, layers, backward, 0)
+    block_gradients(layers - 1)
+    pl.semaphore_wait(barrier, n_shards - 1)
+    start(0, 0)
+    for step in range(1, n_shards):
+        head_copy(step).start()
+    lax.fori_loop(1, layers, backward, 0)
     last = layers - 1
     run(BEFORE_HEAD)
 

time: 68.1 us -> 68.4 us (level)
  no operation moved by 1% of the time
where the time goes in v9:
time: 68.4 us; the launch traced here: 68.3 us
  Pallas kernels  65.7 us (96%)
  between operations  2.58 us (4%)
    pallas_call x1, Pallas kernels, device_step(): pl.pallas_call(functools.partial(step_kernel, n_shards), out_shape=tuple(...  58.6 us
    pallas_call x1, Pallas kernels, device_step(): pl.pallas_call(store_kernel, out_shape=tuple((jax.ShapeDtypeStruct(shape,...  7.13 us

profile of v9, /device:TPU:0, one launch (start us, length us, event | category | flops | bytes accessed | tf_op | source)
XLA Modules:
  0.0 68.3 jit_solution(5610275555717221619)
XLA Ops:
  2.6 58.6 %step_kernel.1 = (f32[8,192,768]{2,1,0:T(8,128)S(1)}, f32[8,192,768]{2,1,0:T(8,128)S(1)}, f32[192,1000]{1,0:T(8,128)S(1)}, f32[8,192,768]{2,1,0:T(8,128)S(1)}, f...) custom-call(bf16[1,192,576]{2,1,0:T(8,128)(2,1)} %bitcast.16, ...), custom_call_target="tpu_custom_call" | custom-call | tf_op jit(solution)/shard_map/step_kernel/pallas_call | solution.py:396
  61.1 7.1 %store_kernel.1 = (f32[8,192,768]{2,1,0:T(8,128)}, f32[8,192,768]{2,1,0:T(8,128)}, f32[192,1000]{1,0:T(8,128)}, f32[8,192,768]{2,1,0:T(8,128)}, f32[8,192,768]{2...) custom-call(f32[1,1]{1,0:T(1,128)} %bitcast.11.rate_ref, f32[1,1]{1,0:T(1,128)} %bitcast.13.coef_ref, ...), custom_call_target="tpu_custom_call" | custom-call | tf_op jit(solution)/shard_map/store_kernel/pallas_call | solution.py:435

commit v10 on v8

--- a/solution.py
+++ b/solution.py
@@ -116,25 +116,22 @@
     small_loads[0].wait()
     stream[...] = x_ref[0].astype(F32).T
 
-    def forward(pair, carry):
-        first = 2 * pair
-        for copy in load(first) + load(first + 1):
-            copy.wait()
-
-        @pl.when(first + 2 < layers)
-        def _():
-            for copy in load(first + 2) + load(first + 3):
-                copy.start()
-
-        @pl.when(first + 2 >= layers)
-        def _():
+    groups = [range(0, 2)] + [range(first, min(first + 3, layers)) for first in range(2, layers, 3)]
+    for number, group in enumerate(groups):
+        for layer in group:
+            for copy in load(layer):
+                copy.wait()
+        if number + 1 < len(groups):
+            for layer in groups[number + 1]:
+                for copy in load(layer):
+                    copy.start()
+        else:
             for copy in small_loads[1:] + [mom_loads[0]]:
                 copy.start()
-
-        for layer in (first, first + 1):
+        for layer in group:
             w_in[layer] = (0.5 * w_in_ref[layer]).astype(BF16)
             w_out[layer] = w_out_ref[layer].astype(BF16)
-        for layer in (first, first + 1):
+        for layer in group:
             for part in parts:
                 stream_in = stream[part]
                 normed, rstd = normalize(stream_in)
@@ -144,9 +141,6 @@
                 pre_acts[layer, part] = pre_half
                 out = (pre_half * gelu_parts(pre_half)[2]).astype(BF16)
                 stream[part] = stream_in + dot(out, w_out[layer], NT)
-        return carry
-
-    lax.fori_loop(0, layers // 2, forward, 0)
     for copy in mom_loads[1:]:
         copy.start()
 
@@ -345,10 +339,10 @@
     old = (w_in_ref, m_in_ref, w_out_ref, m_out_ref)
     new = (w_in_late, m_in_late, w_out_late, m_out_late)
     outs = (w_in_out, m_in_out, w_out_out, m_out_out)
-    copies = [pltpu.make_async_copy(src.at[pl.ds(0, early)], dst.at[pl.ds(0, early)], early_sem.at[i])
-              for i, (src, dst) in enumerate(zip(old, outs))]
-    copies.append(pltpu.make_async_copy(w_head_ref, w_head_out, early_sem.at[4]))
-    copies.append(pltpu.make_async_copy(m_head_ref, m_head_out, early_sem.at[5]))
+    copies = [pltpu.make_async_copy(src.at[layer], dst.at[layer], early_sem.at[3 + 4 * layer + i])
+              for layer in range(early) for i, (src, dst) in enumerate(zip(old, outs))]
+    copies.append(pltpu.make_async_copy(w_head_ref, w_head_out, early_sem.at[0]))
+    copies.append(pltpu.make_async_copy(m_head_ref, m_head_out, early_sem.at[1]))
     for copy in copies:
         copy.start()
     stream[...] = stream_ref[...]
@@ -368,7 +362,7 @@
     pooled = jnp.sum(stream[...], axis=0, keepdims=True) * (1.0 / tokens)
     pooled = jnp.broadcast_to(pooled, (16, dim)).astype(BF16)
     logits[...] = dot(pooled, w_head_ref[...].astype(BF16), NN)[0:1]
-    copies.append(pltpu.make_async_copy(logits, logits_out, early_sem.at[6]))
+    copies.append(pltpu.make_async_copy(logits, logits_out, early_sem.at[2]))
     copies[-1].start()
     for step in range(LATE):
         copies += late_copies(step)
@@ -437,7 +431,7 @@
             scratch_shapes=[
                 pltpu.VMEM((tokens, dim), F32), late, late, late, late,
                 pltpu.VMEM((dim, mlp_dim), BF16), pltpu.VMEM((dim, mlp_dim), BF16), pltpu.VMEM((1, classes), F32),
-                pltpu.SemaphoreType.DMA((7,)), pltpu.SemaphoreType.DMA((LATE, 4)),
+                pltpu.SemaphoreType.DMA((3 + 4 * (layers - LATE),)), pltpu.SemaphoreType.DMA((LATE, 4)),
             ],
             compiler_params=pltpu.CompilerParams(vmem_limit_bytes=11 * 1000 * 1000),
             name="store_kernel",

time: 68.1 us -> 68.3 us (level)
  no operation moved by 1% of the time
where the time goes in v10:
time: 68.3 us; the launch traced here: 68.1 us
  Pallas kernels  65.3 us (96%)
  between operations  2.74 us (4%)
    pallas_call x1, Pallas kernels, device_step(): pl.pallas_call(functools.partial(step_kernel, n_shards), out_shape=tuple(...  58.1 us
    pallas_call x1, Pallas kernels, device_step(): pl.pallas_call(store_kernel, out_shape=tuple((jax.ShapeDtypeStruct(shape,...  7.24 us

profile of v10, /device:TPU:0, one launch (start us, length us, event | category | flops | bytes accessed | tf_op | source)
XLA Modules:
  0.0 68.1 jit_solution(12432872166945618350)
XLA Ops:
  2.6 58.1 %step_kernel.1 = (f32[8,192,768]{2,1,0:T(8,128)S(1)}, f32[8,192,768]{2,1,0:T(8,128)S(1)}, f32[192,1000]{1,0:T(8,128)S(1)}, f32[8,192,768]{2,1,0:T(8,128)S(1)}, f...) custom-call(bf16[1,192,576]{2,1,0:T(8,128)(2,1)} %bitcast.16, ...), custom_call_target="tpu_custom_call" | custom-call | tf_op jit(solution)/shard_map/step_kernel/pallas_call | solution.py:387
  60.7 7.2 %store_kernel.1 = (f32[8,192,768]{2,1,0:T(8,128)}, f32[8,192,768]{2,1,0:T(8,128)}, f32[192,1000]{1,0:T(8,128)}, f32[8,192,768]{2,1,0:T(8,128)}, f32[8,192,768]{2...) custom-call(f32[1,1]{1,0:T(1,128)} %bitcast.11.rate_ref, f32[1,1]{1,0:T(1,128)} %bitcast.13.coef_ref, ...), custom_call_target="tpu_custom_call" | custom-call | tf_op jit(solution)/shard_map/store_kernel/pallas_call | solution.py:426

commit v11 on v8

--- a/solution.py
+++ b/solution.py
@@ -20,7 +20,7 @@
 TN = (((0,), (0,)), ((), ()))
 VMEM_BYTES = 40600 * 1000
 ROWS = 192
-LATE = 3
+LATE = 2
 
 
 def dot(a, b, dims):
@@ -41,12 +41,12 @@
     return square, tanh_val, 1.0 + tanh_val
 
 
-AFTER_BACKWARD = [[], [(0, 0)], [(0, 1)], [(0, 2), (1, 0)], [(1, 1), (0, 3)], [(1, 2), (0, 4)], [(0, 5), (2, 1), (1, 3), (0, 6)], []]
-BEFORE_HEAD = [(1, 5), (0, 7), (2, 3), (1, 6), (2, 5), (1, 4), (1, 7), (2, 2), (2, 6), (2, 0), (2, 4), (2, 7), (3, 5), (3, 6), (3, 7)]
-AFTER_HEAD = [(3, 4), (3, 3), (4, 7), (3, 1), (4, 5), (4, 4), (3, 2), (5, 7), (4, 6)]
-BEFORE_UPDATE = [[], [(5, 4), (5, 5), (3, 0), (5, 6)], [(4, 3), (4, 1)], [(5, 3), (4, 2)], [(4, 0)]]
-AFTER_UPDATE = [[], [], [], [], [(5, 2)]]
-AT_END = [(5, 1), (5, 0)]
+AFTER_BACKWARD = [[], [(0, 0)], [(0, 1)], [(0, 2), (1, 0)], [(1, 1), (0, 3)], [(0, 4)], [(0, 5), (1, 3), (0, 6)], []]
+BEFORE_HEAD = [(1, 2), (0, 7), (1, 5)]
+AFTER_HEAD = [(1, 6), (1, 4), (2, 3), (1, 7), (2, 5), (2, 6), (2, 0), (2, 1), (2, 7), (2, 2), (2, 4), (3, 6), (3, 7), (3, 5), (3, 2), (4, 7), (4, 6), (3, 4), (5, 7)]
+BEFORE_UPDATE = [[], [(3, 0), (3, 1), (4, 5)], [(4, 4), (5, 5)], [(4, 3), (5, 4)], [(5, 3), (4, 0)], [(5, 2)]]
+AFTER_UPDATE = [[(5, 6), (3, 3)], [], [(4, 2)], [], [], [(5, 0), (4, 1)]]
+AT_END = [(5, 1)]
 
 
 def update(layer, slot, rate, coef, sums, old, new, w_in, w_out):
@@ -86,7 +86,7 @@
     chunks = mlp_dim // LANES
     half = chunks * dim
     quarter, eighth = half // 4, half // 8
-    parts = [slice(start, start + ROWS) for start in range(0, tokens, ROWS)]
+    parts = [slice(start, start + tokens // 2) for start in (0, tokens // 2)]
     inner, core = lax.axis_index("inner"), lax.axis_index("data")
     y, x = inner // 2, inner % 2
     peer_core = (inner, 1 - core)

time: 68.1 us -> 67.9 us (level)
  no operation moved by 1% of the time
where the time goes in v11:
time: 67.9 us; the launch traced here: 67.7 us
  Pallas kernels  65.1 us (96%)
  between operations  2.58 us (4%)
    pallas_call x1, Pallas kernels, device_step(): pl.pallas_call(functools.partial(step_kernel, n_shards), out_shape=tuple(...  58 us
    pallas_call x1, Pallas kernels, device_step(): pl.pallas_call(store_kernel, out_shape=tuple((jax.ShapeDtypeStruct(shape,...  7.13 us

profile of v11, /device:TPU:0, one launch (start us, length us, event | category | flops | bytes accessed | tf_op | source)
XLA Modules:
  0.0 67.7 jit_solution(9927166783550143392)
XLA Ops:
  2.6 58.0 %step_kernel.1 = (f32[8,192,768]{2,1,0:T(8,128)S(1)}, f32[8,192,768]{2,1,0:T(8,128)S(1)}, f32[192,1000]{1,0:T(8,128)S(1)}, f32[8,192,768]{2,1,0:T(8,128)S(1)}, f...) custom-call(bf16[1,192,576]{2,1,0:T(8,128)(2,1)} %bitcast.16, ...), custom_call_target="tpu_custom_call" | custom-call | tf_op jit(solution)/shard_map/step_kernel/pallas_call | solution.py:393
  60.6 7.1 %store_kernel.1 = (f32[8,192,768]{2,1,0:T(8,128)}, f32[8,192,768]{2,1,0:T(8,128)}, f32[192,1000]{1,0:T(8,128)}, f32[8,192,768]{2,1,0:T(8,128)}, f32[8,192,768]{2...) custom-call(f32[1,1]{1,0:T(1,128)} %bitcast.11.rate_ref, f32[1,1]{1,0:T(1,128)} %bitcast.13.coef_ref, ...), custom_call_target="tpu_custom_call" | custom-call | tf_op jit(solution)/shard_map/store_kernel/pallas_call | solution.py:432

commit v12 on v11

--- a/solution.py
+++ b/solution.py
@@ -116,25 +116,22 @@
     small_loads[0].wait()
     stream[...] = x_ref[0].astype(F32).T
 
-    def forward(pair, carry):
-        first = 2 * pair
-        for copy in load(first) + load(first + 1):
-            copy.wait()
-
-        @pl.when(first + 2 < layers)
-        def _():
-            for copy in load(first + 2) + load(first + 3):
-                copy.start()
-
-        @pl.when(first + 2 >= layers)
-        def _():
+    groups = [range(0, 2)] + [range(first, min(first + 3, layers)) for first in range(2, layers, 3)]
+    for number, group in enumerate(groups):
+        for layer in group:
+            for copy in load(layer):
+                copy.wait()
+        if number + 1 < len(groups):
+            for layer in groups[number + 1]:
+                for copy in load(layer):
+                    copy.start()
+        else:
             for copy in small_loads[1:] + [mom_loads[0]]:
                 copy.start()
-
-        for layer in (first, first + 1):
+        for layer in group:
             w_in[layer] = (0.5 * w_in_ref[layer]).astype(BF16)
             w_out[layer] = w_out_ref[layer].astype(BF16)
-        for layer in (first, first + 1):
+        for layer in group:
             for part in parts:
                 stream_in = stream[part]
                 normed, rstd = normalize(stream_in)
@@ -144,9 +141,6 @@
                 pre_acts[layer, part] = pre_half
                 out = (pre_half * gelu_parts(pre_half)[2]).astype(BF16)
                 stream[part] = stream_in + dot(out, w_out[layer], NT)
-        return carry
-
-    lax.fori_loop(0, layers // 2, forward, 0)
     for copy in mom_loads[1:]:
         copy.start()
 

time: 67.9 us -> 71.3 us (1.050)
  Pallas kernels: 65.1 us -> 68.4 us
    pallas_call x1, Pallas kernels: 58 us -> 61.2 us  [device_step(): pl.pallas_call(functools.partial(step_kernel, n_shards), out_shape=tuple(...]
where the time goes in v12:
time: 71.3 us; the launch traced here: 71.1 us
  Pallas kernels  68.4 us (96%)
  between operations  2.74 us (4%)
    pallas_call x1, Pallas kernels, device_step(): pl.pallas_call(functools.partial(step_kernel, n_shards), out_shape=tuple(...  61.2 us
    pallas_call x1, Pallas kernels, device_step(): pl.pallas_call(store_kernel, out_shape=tuple((jax.ShapeDtypeStruct(shape,...  7.13 us

profile of v12, /device:TPU:0, one launch (start us, length us, event | category | flops | bytes accessed | tf_op | source)
XLA Modules:
  0.0 71.1 jit_solution(15281425036341380723)
XLA Ops:
  2.6 61.2 %step_kernel.1 = (f32[8,192,768]{2,1,0:T(8,128)S(1)}, f32[8,192,768]{2,1,0:T(8,128)S(1)}, f32[192,1000]{1,0:T(8,128)S(1)}, f32[8,192,768]{2,1,0:T(8,128)S(1)}, f...) custom-call(bf16[1,192,576]{2,1,0:T(8,128)(2,1)} %bitcast.16, ...), custom_call_target="tpu_custom_call" | custom-call | tf_op jit(solution)/shard_map/step_kernel/pallas_call | solution.py:387
  63.8 7.1 %store_kernel.1 = (f32[8,192,768]{2,1,0:T(8,128)}, f32[8,192,768]{2,1,0:T(8,128)}, f32[192,1000]{1,0:T(8,128)}, f32[8,192,768]{2,1,0:T(8,128)}, f32[8,192,768]{2...) custom-call(f32[1,1]{1,0:T(1,128)} %bitcast.11.rate_ref, f32[1,1]{1,0:T(1,128)} %bitcast.13.coef_ref, ...), custom_call_target="tpu_custom_call" | custom-call | tf_op jit(solution)/shard_map/store_kernel/pallas_call | solution.py:426
